TPU v7x, 8 devices: a whole 2x2x1 slice. The times are simulated.
8 devices in a mesh: dp: 1 (over z), eo: 2 (over y), em: 2 (over x), ei: 2 (over core).
Axes of the slice: x: 2, y: 2, z: 1, core: 2. Of those that a mesh axis runs over, the one named last changes fastest.
Arguments:
- x_disp: bfloat16 [8, 64, 192, 2048], P('dp', ('eo', 'em', 'ei'))
- w_gate: bfloat16 [64, 2048, 1408], P(('eo', 'em', 'ei'))
- w_up: bfloat16 [64, 2048, 1408], P(('eo', 'em', 'ei'))
- w_down: bfloat16 [64, 1408, 2048], P(('eo', 'em', 'ei'))
- slot_idx: int32 [8192, 6], P(('dp', 'eo', 'em', 'ei'))
- expert_idx: int32 [8192, 6], P(('dp', 'eo', 'em', 'ei'))
- gate_wt: float32 [8192, 6], P(('dp', 'eo', 'em', 'ei'))
Outputs:
- output: bfloat16 [8192, 2048], P(('dp', 'eo', 'em', 'ei'))
All inputs are finite; a program needn't handle non-finite values.
Results may differ from a plain program's by a relative error of at most 0.00136.
Values are sent between devices in bfloat16 or wider.
A program may use at most 1 GiB of HBM per device.

v0:
```python
import jax
import jax.numpy as jnp
from jax import lax
from jax.sharding import PartitionSpec as P

GROUP_AXES = ('eo', 'em', 'ei')


def combine_rows(flat_rows, slot_idx, expert_idx, gate_wt, slot_count):
    is_live = slot_idx >= 0
    row_index = jnp.where(is_live, expert_idx * slot_count + slot_idx, 0)
    weight = jnp.where(is_live, gate_wt, 0.0)
    picked = jnp.take(flat_rows, row_index, axis=0)
    combined = jnp.sum(weight[:, :, None] * picked.astype(jnp.float32), axis=1)
    return combined.astype(jnp.bfloat16)


def solution(mesh):
    token_spec = P(('dp',) + GROUP_AXES, None)
    weight_spec = P(GROUP_AXES, None, None)
    rows_spec = P('dp', GROUP_AXES, None, None)

    def local_part(x_local, w_gate, w_up, w_down, slot_idx, expert_idx, gate_wt):
        slot_count = x_local.shape[2]
        model_width = x_local.shape[3]
        gate_pre = jnp.einsum('secd,edf->escf', x_local, w_gate, preferred_element_type=jnp.float32)
        up_pre = jnp.einsum('secd,edf->escf', x_local, w_up, preferred_element_type=jnp.float32)
        hidden = (jax.nn.silu(gate_pre) * up_pre).astype(jnp.bfloat16)
        y_rows = jnp.einsum('escf,efd->escd', hidden, w_down, preferred_element_type=jnp.float32).astype(jnp.bfloat16)
        returned = lax.all_to_all(y_rows, GROUP_AXES, 1, 0, tiled=True)
        flat_rows = returned.reshape(-1, model_width)
        return combine_rows(flat_rows, slot_idx, expert_idx, gate_wt, slot_count)

    return jax.shard_map(local_part, mesh=mesh,
                         in_specs=(rows_spec, weight_spec, weight_spec, weight_spec, token_spec, token_spec, token_spec),
                         out_specs=token_spec, check_vma=False)
```

profile of v0, /device:TPU:0, one launch (start us, length us, event | category | flops | bytes accessed | tf_op | source)
XLA Modules:
  0.0 1137.0 jit_solution(9696509519399165176)
XLA Ops:
  0.0 87.8 %fusion.2 = f32[8,8,192,1408]{3,2,1,0:T(8,128)} fusion(bf16[8,2048,1408]{2,1,0:T(8,128)(2,1)} %param.9, bf16[8,8,192,2048]{3,2,1,0:T(8,128)(2,1)} %param.7), kind=kOutput, calls=%fused_computation.5 | convolution fusion | flops 70866960384 | bytes 165675008 | tf_op jit(solution)/shard_map/secd,edf->escf/dot_general | solution.py:27
  87.8 98.3 %multiply_convert_fusion = bf16[8,8,192,1408]{3,2,1,0:T(8,128)(2,1)} fusion(f32[8,8,192,1408]{3,2,1,0:T(8,128)} %fusion.2, bf16[8,2048,1408]{2,1,0:T(8,128)(2,1)} %param.8, bf16[8,8,192,2048]{3,2,1,0:T(8,128)(2,1)} %param.7), kind=kOutput, calls=%fused_computation.1 | convolution fusion | flops 70970769408 | bytes 200278016 | tf_op jit(solution)/shard_map/secd,edf->escf/dot_general | solution.py:26
  186.1 87.8 %fusion.7 = bf16[8,8,192,2048]{3,2,1,0:T(8,128)(2,1)} fusion(bf16[8,8,192,1408]{3,2,1,0:T(8,128)(2,1)} %multiply_convert_fusion, bf16[8,1408,2048]{2,1,0:T(8,128)(2,1)} %param.10), kind=kOutput, calls=%fused_computation.10 | convolution fusion | flops 70892126208 | bytes 131072000 | tf_op jit(solution)/shard_map/escf,efd->escd/dot_general | solution.py:29
  273.9 33.5 %copy.20 = bf16[8,8,192,2048]{3,2,0,1:T(8,128)(2,1)} copy(bf16[8,8,192,2048]{3,2,1,0:T(8,128)(2,1)} %fusion.7) | data formatting | bytes 100663296 | tf_op jit(solution)/shard_map/convert_element_type | solution.py:29
  307.4 0.0 copy-start
  307.4 0.0 copy-start.2
  307.4 0.0 copy-start.1
  307.4 7.6 all-to-all-start
  315.0 0.0 copy-done
  315.0 0.0 copy-done.2
  315.1 0.2 copy.21
  315.3 0.3 reshape.13
  315.6 0.0 copy-done.1
  315.7 0.2 copy.16
  315.9 0.3 copy.17
  316.2 543.6 %all-to-all-done = bf16[8,8,192,2048]{3,2,0,1:T(8,128)(2,1)} async-done(((bf16[8,8,192,2048]{3,2,0,1:T(8,128)(2,1)}), bf16[8,8,192,2048]{3,2,0,1:T(8,128)(2,1)}, u32[]{:S(2)}, u32[]{:S(2)}) %all-to-all-start) | async-done | bytes 50331680 | tf_op jit(solution)/shard_map/all_to_all | solution.py:30
  859.8 198.7 %gather_fusion = bf16[6144,2048]{1,0:T(8,128)(2,1)} fusion(bf16[12288,2048]{1,0:T(8,128)(2,1)} %bitcast.8, s32[6144]{0:T(1024)S(1)} %broadcast_clamp_fusion), kind=kCustom, calls=%fused_computation | custom fusion | bytes 50356224 | tf_op jit(solution)/shard_map/jit(_take)/gather | solution.py:13
  1058.6 39.4 %reshape.12 = bf16[1024,6,2048]{2,1,0:T(8,128)(2,1)} reshape(bf16[6144,2048]{1,0:T(8,128)(2,1)} %gather_fusion) | data formatting | bytes 50331648 | tf_op jit(solution)/shard_map/jit(_take)/gather | solution.py:13
  1098.0 39.0 %multiply_reduce_fusion = bf16[1024,2048]{1,0:T(8,128)(2,1)} fusion(bf16[1024,6,2048]{2,1,0:T(8,128)(2,1)} %reshape.12, f32[1024,6]{1,0:T(8,128)S(1)} %copy.16, pred[1024,6]{1,0:T(8,128)(4,1)S(1)} %copy.17), kind=kLoop, calls=%fused_computation.2 | loop fusion | flops 48234496 | bytes 29390848 | tf_op jit(solution)/shard_map/reduce_sum | solution.py:14
  (3 shorter events, 0.0 us)
Async XLA Ops:
  307.4 7.6 copy-start
  307.4 7.7 copy-start.2
  307.4 8.3 copy-start.1
  307.4 552.4 %all-to-all-start = ((bf16[8,8,192,2048]{3,2,0,1:T(8,128)(2,1)}), bf16[8,8,192,2048]{3,2,0,1:T(8,128)(2,1)}, u32[]{:S(2)}, u32[]{:S(2)}) async-start(bf16[8,8,192,2048]{3,2,0,1:T(8,128)(2,1)} %copy.20), calls=%async_computation | async-start | bytes 100663296 | tf_op jit(solution)/shard_map/all_to_all | solution.py:30
where the time goes:
time: 1140 us
  waiting for transfers between devices  544 us (48%)
  matrix products  274 us (24%)
  local copies, waits for them, and re-layouts  273 us (24%)
  other arithmetic  39 us (3%)
    all_to_all x1, waiting for transfers between devices, local_part(): returned = lax.all_to_all(y_rows, GROUP_AXES, 1, 0, tiled=True)  544 us
    gather x2, local copies, waits for them, and re-layouts, combine_rows(): picked = jnp.take(flat_rows, row_index, axis=0)  238 us
    dot_general x1, matrix products, local_part(): jnp.einsum('secd,edf->escf', x_local, w_gate, preferred_element_type=jnp....  98.3 us
    dot_general x1, matrix products, local_part(): jnp.einsum('secd,edf->escf', x_local, w_up, preferred_element_type=jnp.fl...  87.8 us
    dot_general x1, matrix products, local_part(): jnp.einsum('escf,efd->escd', hidden, w_down, preferred_element_type=jnp.f...  87.8 us
    reduce_sum x1, other arithmetic, combine_rows(): combined = jnp.sum(weight[:, :, None] * picked.astype(jnp.float32), axis=1)  39 us
    convert_element_type x1, local copies, waits for them, and re-layouts, local_part(): jnp.einsum('escf,efd->escd', hidden, w_down, preferred_element_type=jnp.f...  33.5 us
  transfers between devices with their start and end apart: 1, of which 1 were waited for; matrix products, arithmetic and copies ran while one was open for 0% of the time, Pallas kernels for 0%

commit v1 on v0

v1 whole, which is shorter than its diff:
```python
import functools

import jax
import jax.numpy as jnp
from jax import lax
from jax.experimental import pallas as pl
from jax.experimental.pallas import tpu as pltpu
from jax.sharding import PartitionSpec as P


GROUP_AXES = ('eo', 'em', 'ei')
LANES = 128
COLS = 1024
JT = COLS // LANES
ANY = pl.ANY


def slot_tables(slot_idx, expert_idx, gate_wt, n_exp, n_slot):
    n_tok, top = slot_idx.shape
    tok = lax.broadcasted_iota(jnp.int32, (n_tok, top), 0)
    spare = float(n_tok * JT)
    delta = (tok * JT).astype(jnp.float32) - spare
    exp_hot = (expert_idx[:, :, None] == lax.broadcasted_iota(jnp.int32, (1, 1, n_exp), 2)).astype(jnp.float32)
    slot_hot = (slot_idx[:, :, None] == lax.broadcasted_iota(jnp.int32, (1, 1, n_slot), 2)).astype(jnp.float32)
    both = jnp.concatenate([exp_hot * delta[:, :, None], exp_hot * gate_wt[:, :, None]], axis=2)
    table = jnp.einsum('tje,tjc->ec', both, slot_hot, precision=lax.Precision.HIGHEST,
                       preferred_element_type=jnp.float32)
    addr, wt = table[:n_exp] + spare, table[n_exp:]
    return jnp.stack([addr, wt])


def round16(n):
    return (n + 15) // 16 * 16


def row_chunks(total, body):
    whole = (total + 127) // 256
    rest = total - whole * 256

    def chunk(c, carry):
        body(pl.multiple_of(c * 256, 256), 256)
        return carry

    lax.fori_loop(0, whole, chunk, 0)
    pl.when(rest > 0)(lambda: body(pl.multiple_of(whole * 256, 256), 128))


def gate_up_tile(x, wg_ref, wu_ref, cols):
    w = jnp.concatenate([wg_ref[0, :, cols], wu_ref[0, :, cols]], axis=1)
    gu = jnp.dot(x, w, preferred_element_type=jnp.float32)
    g, u = gu[:, :LANES], gu[:, LANES:]
    return ((g * jax.nn.sigmoid(g)) * u).astype(jnp.bfloat16)


def gate_up_full_kernel(q_ref, x_ref, wg_ref, wu_ref, h_ref):
    _, _, slots, width = x_ref.shape
    for j in range(wg_ref.shape[2] // LANES):
        cols = slice(j * LANES, (j + 1) * LANES)
        h_ref[0, :, cols] = gate_up_tile(x_ref[...].reshape(2 * slots, width), wg_ref, wu_ref, cols)


def gate_up_full(q, x, wg, wu):
    _, n_exp, slots, width = x.shape
    ff = wg.shape[2]
    return pl.pallas_call(
        gate_up_full_kernel,
        grid_spec=pltpu.PrefetchScalarGridSpec(
            num_scalar_prefetch=1, grid=(n_exp,),
            in_specs=[pl.BlockSpec((2, 1, slots, width), lambda e, q: (q[0], e, 0, 0))] +
                     [pl.BlockSpec((1, width, ff), lambda e, q: (e, 0, 0))] * 2,
            out_specs=pl.BlockSpec((1, 2 * slots, ff), lambda e, q: (e, 0, 0))),
        out_shape=jax.ShapeDtypeStruct((n_exp, 2 * slots, ff), jnp.bfloat16),
        compiler_params=pltpu.CompilerParams(dimension_semantics=('arbitrary',), vmem_limit_bytes=60 * 2 ** 20),
        cost_estimate=pl.CostEstimate(flops=2 * n_exp * 2 * slots * width * ff * 2, transcendentals=0,
                                      bytes_accessed=n_exp * width * ff * 4),
        name='gate_up_full',
    )(q, x, wg, wu)


def gate_up_kernel(n_q, q_ref, n_ref, *refs):
    x_refs, (wg_ref, wu_ref), (h_ref, xs_ref) = refs[:n_q], refs[n_q:n_q + 2], refs[-2:]
    e = pl.program_id(0)
    n_exp = pl.num_programs(0)
    ff = wg_ref.shape[2]

    first = jnp.int32(0)
    for g in range(n_q):
        for i in range(2):
            rows = round16(n_ref[(2 * q_ref[g] + i) * n_exp + e])
            at = first

            def copy(b, carry):
                xs_ref[pl.ds(pl.multiple_of(at + b * 16, 16), 16), :] = (
                    x_refs[g][i, 0, pl.ds(pl.multiple_of(b * 16, 16), 16), :])
                return carry

            lax.fori_loop(0, rows // 16, copy, 0)
            first = first + rows

    def body(r0, rows):
        r = pl.ds(r0, rows)
        for j in range(ff // LANES):
            cols = slice(j * LANES, (j + 1) * LANES)
            h_ref[0, r, cols] = gate_up_tile(xs_ref[r, :], wg_ref, wu_ref, cols)

    row_chunks(first, body)


def gate_up(qs, count, x, wg, wu, after):
    _, n_exp, slots, width = x.shape
    ff = wg.shape[2]
    n_q = qs.shape[0]
    rows = n_q * 2 * slots

    def x_spec(g):
        return pl.BlockSpec((2, 1, slots, width), lambda e, q, c: (q[g], e, 0, 0))

    return pl.pallas_call(
        functools.partial(gate_up_kernel, n_q),
        grid_spec=pltpu.PrefetchScalarGridSpec(
            num_scalar_prefetch=2, grid=(n_exp,),
            in_specs=[x_spec(g) for g in range(n_q)] +
                     [pl.BlockSpec((1, width, ff), lambda e, q, c: (e, 0, 0))] * 2 +
                     [pl.BlockSpec(memory_space=ANY)] * len(after),
            out_specs=pl.BlockSpec((1, rows, ff), lambda e, q, c: (e, 0, 0)),
            scratch_shapes=[pltpu.VMEM((rows, width), jnp.bfloat16)]),
        out_shape=jax.ShapeDtypeStruct((n_exp, rows, ff), jnp.bfloat16),
        compiler_params=pltpu.CompilerParams(dimension_semantics=('arbitrary',), vmem_limit_bytes=60 * 2 ** 20),
        cost_estimate=pl.CostEstimate(flops=2 * n_exp * rows * width * ff * 2, transcendentals=0,
                                      bytes_accessed=n_exp * width * ff * 4),
        name='gate_up',
    )(qs, count, *[x] * n_q, wg, wu, *after)


def down_combine_kernel(n_q, packed, q_ref, core_ref, n_ref, *refs):
    addr_refs, wt_refs, (h_ref, wd_ref), rest = refs[:n_q], refs[n_q:2 * n_q], refs[2 * n_q:2 * n_q + 2], refs[2 * n_q + 2:]
    outs, (acc_ref, y_ref, sem) = rest[-3 - 2 * n_q:-3], rest[-3:]
    e = pl.program_id(0)
    n_exp = pl.num_programs(0)
    n_acc = 2 * n_q
    slots = h_ref.shape[1] // n_acc

    @pl.when(e == 0)
    def _():
        def zero(i, carry):
            z = jnp.zeros((8 * JT, LANES), jnp.float32)
            r = pl.ds(pl.multiple_of(i * 8 * JT, 8 * JT), 8 * JT)
            for k in range(n_acc):
                acc_ref[k, r, :] = z
            return carry

        lax.fori_loop(0, acc_ref.shape[1] // (8 * JT), zero, 0)

    starts, counts = [], []
    first = jnp.int32(0)
    for g in range(n_q):
        for i in range(2):
            n = n_ref[(2 * q_ref[g] + i) * n_exp + e]
            starts.append(first)
            counts.append(n)
            first = first + (round16(n) if packed else slots)

    def body(r0, rows):
        for jj in range(COLS // 256):
            y = jnp.dot(h_ref[0, pl.ds(r0, rows), :], wd_ref[0, :, jj * 256:(jj + 1) * 256],
                        preferred_element_type=jnp.float32)
            y = y.astype(jnp.bfloat16).astype(jnp.float32)
            for k in range(2):
                y_ref[pl.ds(r0 // 8, rows // 8), (jj * 2 + k) * 8:(jj * 2 + k + 1) * 8, :] = (
                    y[:, k * LANES:(k + 1) * LANES].reshape(rows // 8, 8, LANES))

    if packed:
        row_chunks(first, body)
    else:
        body(0, n_acc * slots)

    for g in range(n_q):
        for i in range(2):
            k_acc = 2 * g + i
            y0 = starts[k_acc] // 8
            acc = acc_ref.at[k_acc]

            def batch(b, carry):
                ks = range(16)
                addrs = [addr_refs[g][0, 0, 0, i * slots + b * 16 + k] for k in ks]
                wts = [wt_refs[g][0, 0, 0, i * slots + b * 16 + k] for k in ks]
                ys = [y_ref[y0 + b * 2 + k // 8, pl.ds(k % 8, JT, stride=8), :] for k in ks]
                at = [pl.ds(pl.multiple_of(addrs[k], JT), JT) for k in ks]
                old = [acc[at[k], :] for k in ks]
                for k in ks:
                    acc[at[k], :] = old[k] + wts[k] * ys[k]
                return carry

            lax.fori_loop(0, (counts[k_acc] + 15) // 16, batch, 0)

    @pl.when(e == n_exp - 1)
    def _():
        copies = []
        for g in range(n_q):
            for i in range(2):
                own = core_ref[0] == i
                for dst, cond in ((outs[2 * g], own), (outs[2 * g + 1], jnp.logical_not(own))):
                    copy = pltpu.make_async_copy(acc_ref.at[2 * g + i], dst, sem.at[2 * g + i])
                    pl.when(cond)(copy.start)
                copies.append(copy)
        for copy in copies:
            copy.wait()


def down_combine(qs, core, addr, wt, count, h, wd, n, n_tok, slots, packed, after):
    n_exp, rows, ff = h.shape
    n_q = qs.shape[0]
    acc_rows = (n_tok + 8) * JT
    acc = jax.ShapeDtypeStruct((acc_rows, LANES), jnp.float32)

    def table_spec(g):
        return pl.BlockSpec((1, 1, 1, 2 * slots), lambda e, q, *_: (q[g], e, 0, 0), memory_space=pltpu.SMEM)

    return pl.pallas_call(
        functools.partial(down_combine_kernel, n_q, packed),
        grid_spec=pltpu.PrefetchScalarGridSpec(
            num_scalar_prefetch=3, grid=(n_exp,),
            in_specs=[table_spec(g) for g in range(n_q)] * 2 +
                     [pl.BlockSpec((1, rows, ff), lambda e, *_: (e, 0, 0)),
                      pl.BlockSpec((1, ff, COLS), lambda e, *_: (e, 0, n))] +
                     [pl.BlockSpec(memory_space=ANY)] * len(after),
            out_specs=[pl.BlockSpec(memory_space=ANY)] * (2 * n_q),
            scratch_shapes=[pltpu.VMEM((2 * n_q, acc_rows, LANES), jnp.float32),
                            pltpu.VMEM((rows // 8, 8 * JT, LANES), jnp.float32),
                            pltpu.SemaphoreType.DMA((2 * n_q,))]),
        out_shape=[acc] * (2 * n_q),
        compiler_params=pltpu.CompilerParams(dimension_semantics=('arbitrary',), vmem_limit_bytes=60 * 2 ** 20),
        cost_estimate=pl.CostEstimate(flops=2 * n_exp * rows * ff * COLS, transcendentals=0,
                                      bytes_accessed=n_exp * COLS * ff * 2 + 2 * n_q * acc_rows * LANES * 4),
        name='down_combine',
    )(qs, core, count, *[addr] * n_q, *[wt] * n_q, h, wd, *after)


def final_kernel(a1_ref, a2_ref, b1_ref, b2_ref, *rest):
    out_ref, s_ref = rest[-2:]
    step = pl.program_id(0)
    half = pl.num_programs(0) // 2

    def emit(a_ref, b_ref):
        def body(b, carry):
            r = pl.ds(pl.multiple_of(b * 16 * JT, 16 * JT), 16 * JT)
            s_ref[r, :] = a_ref[r, :] + b_ref[r, :]
            for j in range(JT):
                pair = [s_ref[pl.ds((b * 16 + k) * JT + j, 8, stride=JT), :] for k in (0, 8)]
                out_ref[pl.ds(pl.multiple_of(b * 16, 16), 16), j * LANES:(j + 1) * LANES] = (
                    jnp.concatenate(pair, axis=0).astype(out_ref.dtype))
            return carry

        lax.fori_loop(0, out_ref.shape[0] // 16, body, 0)

    pl.when(step < half)(lambda: emit(a1_ref, b1_ref))
    pl.when(step >= half)(lambda: emit(a2_ref, b2_ref))


def final_sum(a1, a2, b1, b2, n, n_tok, width, out):
    tb = 128
    steps = n_tok // tb
    half = steps // 2
    low = pl.BlockSpec((tb * JT, LANES), lambda i: (jnp.minimum(i, half - 1), 0))
    high = pl.BlockSpec((tb * JT, LANES), lambda i: (jnp.maximum(i - half, 0), 0))
    prior = [] if out is None else [out]
    return pl.pallas_call(
        final_kernel,
        grid=(steps,),
        in_specs=[low, high, low, high] + [pl.BlockSpec(memory_space=ANY)] * len(prior),
        out_specs=pl.BlockSpec((tb, COLS), lambda i: (i, n)),
        scratch_shapes=[pltpu.VMEM((tb * JT, LANES), jnp.float32)],
        out_shape=jax.ShapeDtypeStruct((n_tok, width), jnp.bfloat16),
        input_output_aliases={4: 0} if prior else {},
        compiler_params=pltpu.CompilerParams(dimension_semantics=('arbitrary',), vmem_limit_bytes=30 * 2 ** 20),
        cost_estimate=pl.CostEstimate(flops=10 ** 7, transcendentals=0, bytes_accessed=n_tok * COLS * 10),
        name='final_sum',
    )(a1, a2, b1, b2, *prior)


def solution(mesh):
    token_spec = P(('dp',) + GROUP_AXES, None)
    weight_spec = P(GROUP_AXES, None, None)
    rows_spec = P('dp', GROUP_AXES, None, None)
    n_dev = mesh.shape['eo'] * mesh.shape['em'] * mesh.shape['ei']
    core_bit, x_bit, y_bit = 1, 2, 4

    def swap(a, bit):
        return lax.ppermute(a, GROUP_AXES, [(i, i ^ bit) for i in range(n_dev)])

    def local_part(x_local, w_gate, w_up, w_down, slot_idx, expert_idx, gate_wt):
        _, n_exp, slots, width = x_local.shape
        n_tok = slot_idx.shape[0]
        n_cb = width // COLS
        core = lax.axis_index('ei').astype(jnp.int32).reshape(1)
        chip = (lax.axis_index('eo') * 2 + lax.axis_index('em')).astype(jnp.int32)

        table = slot_tables(slot_idx, expert_idx, gate_wt, n_dev * n_exp, slots)
        table = table.reshape(2, n_dev, n_exp, slots).swapaxes(0, 1)
        table = lax.all_to_all(table, GROUP_AXES, 0, 0, tiled=True)
        addr = table[:, 0].astype(jnp.int32)
        wt = table[:, 1]
        seen = jnp.where(wt > 0, lax.broadcasted_iota(jnp.int32, wt.shape, 2) + 1, 0)
        count = jnp.max(seen, axis=2).reshape(-1)

        def by_chip(a):
            return a.reshape(n_dev // 2, 2, n_exp, slots).swapaxes(1, 2).reshape(n_dev // 2, n_exp, 1, 2 * slots)

        addr, wt = by_chip(addr), by_chip(wt)

        lo, hi = slice(0, n_tok // 2 * JT), slice(n_tok // 2 * JT, n_tok * JT)
        blocks = range(n_cb)

        def ffn(flips, packed, after):
            qs = jnp.stack([chip ^ f for f in flips])
            if packed:
                h = gate_up(qs, count, x_local, w_gate, w_up, after)
            else:
                h = gate_up_full(qs, x_local, w_gate, w_up)
            outs = []
            prev = []
            for n in blocks:
                accs = down_combine(qs, core, addr, wt, count, h, w_down, n, n_tok, slots, packed, prev)
                outs.append([(accs[2 * g], swap(accs[2 * g + 1], core_bit))
                             for g in range(len(flips))])
                prev = [accs[0]]
            return outs

        diag = ffn([3], False, [])
        relay_x, relay_y, gate = [], [], []
        for n in blocks:
            (own, sib), = diag[n]
            first, second = own[lo] + sib[lo], own[hi] + sib[hi]
            relay_x.append(swap(first, x_bit))
            relay_y.append(swap(second, y_bit))
            gate.append(first)

        near = ffn([1, 2], True, gate)
        x1, x2, y1, y2 = [], [], [], []
        for n in blocks:
            (own_x, sib_x), (own_y, sib_y) = near[n]
            x1.append(swap(own_x[lo] + sib_x[lo], x_bit))
            y2.append(swap(own_y[hi] + sib_y[hi], y_bit))
            own_x, sib_x, own_y, sib_y, from_x, from_y = lax.optimization_barrier(
                (own_x, sib_x, own_y, sib_y, relay_x[n], relay_y[n]))
            x2.append(swap(own_x[hi] + sib_x[hi] + from_y, x_bit))
            y1.append(swap(own_y[lo] + sib_y[lo] + from_x, y_bit))

        here = ffn([0], True, [near[-1][0][0]])
        out = None
        for n in blocks:
            (own, sib), = here[n]
            a1 = own[lo] + sib[lo] + x1[n]
            a2 = own[hi] + sib[hi] + y2[n]
            out = final_sum(a1, a2, y1[n], x2[n], n, n_tok, width, out)
        return out

    return jax.shard_map(local_part, mesh=mesh,
                         in_specs=(rows_spec, weight_spec, weight_spec, weight_spec, token_spec, token_spec, token_spec),
                         out_specs=token_spec, check_vma=False)
```

time: 1140 us -> 574 us (0.50)
  waiting for transfers between devices: 544 us -> 186 us
  Pallas kernels: 0 us -> 298 us
  matrix products: 274 us -> 3.18 us
  local copies, waits for them, and re-layouts: 273 us -> 5.76 us
  starting transfers between devices: 7.61 us -> 32.4 us
    all_to_all x1, waiting for transfers between devices: 544 us -> 0.01 us  [local_part(): table = lax.all_to_all(table, GROUP_AXES, 0, 0, tiled=True)]
    pallas_call x0 -> x11, Pallas kernels: none -> 298 us  [the longest x6 149 us: down_combine(): pl.pallas_call(functools.partial(down_combine_kernel, n_q, packed), grid_...]
    dot_general x3 -> x1, matrix products: 274 us -> 3.18 us  [slot_tables(): jnp.einsum('tje,tjc->ec', both, slot_hot, precision=lax.Precision.HIGHEST...]
    gather x2 -> x0, local copies, waits for them, and re-layouts: 238 us -> none  [combine_rows(): picked = jnp.take(flat_rows, row_index, axis=0)]
    ppermute x0 -> x20, waiting for transfers between devices: none -> 186 us  [swap(): return lax.ppermute(a, GROUP_AXES, [(i, i ^ bit) for i in range(n_dev)])]
    add x0 -> x13, other arithmetic: none -> 44.4 us  [the longest x2 11 us: local_part(): first, second = (own[lo] + sib[lo], own[hi] + sib[hi])]
    reduce_sum x1 -> x0, other arithmetic: 39 us -> none  [combine_rows(): combined = jnp.sum(weight[:, :, None] * picked.astype(jnp.float32), axis=1)]
    convert_element_type x1 -> x0, local copies, waits for them, and re-layouts: 33.5 us -> none  [local_part(): jnp.einsum('escf,efd->escd', hidden, w_down, preferred_element_type=jnp.f...]
  transfers between devices with their start and end apart: 1 -> 21, of which waited for: 1 -> 6; matrix products, arithmetic and copies ran while one was open for 0% -> 8% of each run, Pallas kernels for 0% -> 47%
where the time goes in v1:
time: 574 us
  Pallas kernels  298 us (52%)
  waiting for transfers between devices  186 us (32%)
  other arithmetic  47.9 us (8%)
  starting transfers between devices  32.4 us (6%)
  local copies, waits for them, and re-layouts  5.76 us (1%)
    ppermute x20, waiting for transfers between devices, swap(): return lax.ppermute(a, GROUP_AXES, [(i, i ^ bit) for i in range(n_dev)])  186 us
    pallas_call x6, Pallas kernels, down_combine(): pl.pallas_call(functools.partial(down_combine_kernel, n_q, packed), grid_...  149 us
    pallas_call x2, Pallas kernels, gate_up(): pl.pallas_call(functools.partial(gate_up_kernel, n_q), grid_spec=pltpu.Pr...  97.1 us
    pallas_call x1, Pallas kernels, gate_up_full(): pl.pallas_call(gate_up_full_kernel, grid_spec=pltpu.PrefetchScalarGridSpe...  44.7 us
    ppermute x20, starting transfers between devices, swap(): return lax.ppermute(a, GROUP_AXES, [(i, i ^ bit) for i in range(n_dev)])  28.2 us
  transfers between devices with their start and end apart: 21, of which 6 were waited for; matrix products, arithmetic and copies ran while one was open for 8% of the time, Pallas kernels for 47%

profile of v1, /device:TPU:0, one launch (start us, length us, event | category | flops | bytes accessed | tf_op | source)
XLA Modules:
  0.0 573.6 jit_solution(3573962875526218834)
XLA Ops:
  0.0 2.7 fusion.5
  2.7 3.2 fusion.11
  6.2 0.7 copy.22
  6.8 4.3 all-to-all-start
  11.1 44.7 %gate_up_full.1.refs_2_ = bf16[8,384,1408]{2,1,0:T(8,128)(2,1)} custom-call(s32[1]{0:T(128)} %bitcast.13.q_ref, bf16[8,8,192,2048]{3,2,1,0:T(8,128)(2,1)} %refs_0_.3, bf16[8,2048,1408]{2,1,0:T(8,128)(2,1)} %refs_1_.3, bf16[8,2048,1408]{2,1,0:T(8,128)(2,1)} %refs_2_.3), custom_call_target="tpu_custom_call" | custom-call | flops 35433480192 | bytes 92274688 | tf_op jit(solution)/shard_map/gate_up_full/pallas_call | solution.py:65
  56.1 0.7 reshape.31.n_ref
  56.8 0.8 reshape.32.refs_0_.refs_1_
  57.6 0.7 reshape.33.refs_1_.refs_2_.refs_3_
  58.4 22.7 %down_combine.6 = (f32[8256,128]{1,0:T(8,128)}, f32[8256,128]{1,0:T(8,128)}) custom-call(s32[1]{0:T(128)} %bitcast.13.q_ref, s32[1]{0:T(128)} %bitcast.1.core_ref, s32[64]{0:T(128)} %reshape.31.n_ref, s32[4,8,1,384]{3,2,1,0:T(1,128)} %reshape.32.refs_0_.refs_1_, f32[4,8,1,384]{3,2,1,0:T(1,128)} %reshape.33.refs_1_.refs_2_.refs_3_, ...), custom_call_target="tpu_custom_call" | custom-call | flops 8858370048 | bytes 31522816 | tf_op jit(solution)/shard_map/down_combine/pallas_call | solution.py:219
  81.0 1.0 collective-permute-start
  82.0 22.6 %down_combine.7 = (f32[8256,128]{1,0:T(8,128)}, f32[8256,128]{1,0:T(8,128)}) custom-call(s32[1]{0:T(128)} %bitcast.13.q_ref, s32[1]{0:T(128)} %bitcast.1.core_ref, s32[64]{0:T(128)} %reshape.31.n_ref, s32[4,8,1,384]{3,2,1,0:T(1,128)} %reshape.32.refs_0_.refs_1_, f32[4,8,1,384]{3,2,1,0:T(1,128)} %reshape.33.refs_1_.refs_2_.refs_3_, ...), custom_call_target="tpu_custom_call" | custom-call | flops 8858370048 | bytes 31522816 | tf_op jit(solution)/shard_map/down_combine/pallas_call | solution.py:219
  104.6 0.6 collective-permute-start.1
  105.2 0.6 pad_add_fusion.q_ref
  105.8 6.2 %slice_add_fusion = (f32[4096,128]{1,0:T(8,128)}, f32[4096,128]{1,0:T(8,128)}) fusion(f32[8256,128]{1,0:T(8,128)} %collective-permute-done, f32[8256,128]{1,0:T(8,128)} %get-tuple-element.33.refs_4_), kind=kLoop, calls=%fused_computation.9 | loop fusion | flops 1048576 | bytes 12582912 | tf_op jit(solution)/shard_map/add | solution.py:333
  112.0 2.5 collective-permute-start.16
  114.5 4.8 slice_add_fusion.5
  119.3 57.1 %gate_up.2.refs_4_ = bf16[8,768,1408]{2,1,0:T(8,128)(2,1)} custom-call(s32[2]{0:T(128)} %pad_add_fusion.q_ref, s32[64]{0:T(128)} %reshape.31.n_ref, bf16[8,8,192,2048]{3,2,1,0:T(8,128)(2,1)} %refs_0_.3, bf16[8,8,192,2048]{3,2,1,0:T(8,128)(2,1)} %refs_0_.3, bf16[8,2048,1408]{2,1,0:T(8,128)(2,1)} %refs_1_.3, bf16[8,2048,1408]{2,1,0:T(8,128)(2,1)} %refs_2_.3, ...), custom_call_target="tpu_custom_call" | custom-call | flops 70866960384 | bytes 92274688 | tf_op jit(solution)/shard_map/gate_up/pallas_call | solution.py:118
  176.4 31.3 %down_combine.8 = (f32[8256,128]{1,0:T(8,128)}, f32[8256,128]{1,0:T(8,128)}, f32[8256,128]{1,0:T(8,128)}, f32[8256,128]{1,0:T(8,128)}) custom-call(s32[2]{0:T(128)} %pad_add_fusion.q_ref, s32[1]{0:T(128)} %bitcast.1.core_ref, s32[64]{0:T(128)} %reshape.31.n_ref, s32[4,8,1,384]{3,2,1,0:T(1,128)} %reshape.32.refs_0_.refs_1_, ...), custom_call_target="tpu_custom_call" | custom-call | flops 17716740096 | bytes 39976960 | tf_op jit(solution)/shard_map/down_combine/pallas_call | solution.py:219
  207.7 4.6 collective-permute-start.12
  212.4 31.0 %down_combine.9 = (f32[8256,128]{1,0:T(8,128)}, f32[8256,128]{1,0:T(8,128)}, f32[8256,128]{1,0:T(8,128)}, f32[8256,128]{1,0:T(8,128)}) custom-call(s32[2]{0:T(128)} %pad_add_fusion.q_ref, s32[1]{0:T(128)} %bitcast.1.core_ref, s32[64]{0:T(128)} %reshape.31.n_ref, s32[4,8,1,384]{3,2,1,0:T(1,128)} %reshape.32.refs_0_.refs_1_, ...), custom_call_target="tpu_custom_call" | custom-call | flops 17716740096 | bytes 39976960 | tf_op jit(solution)/shard_map/down_combine/pallas_call | solution.py:219
  243.4 3.0 collective-permute-start.3
  246.4 40.0 %gate_up.3.refs_2_ = bf16[8,384,1408]{2,1,0:T(8,128)(2,1)} custom-call(s32[1]{0:T(128)} %bitcast.q_ref, s32[64]{0:T(128)} %reshape.31.n_ref, bf16[8,8,192,2048]{3,2,1,0:T(8,128)(2,1)} %refs_0_.3, bf16[8,2048,1408]{2,1,0:T(8,128)(2,1)} %refs_1_.3, bf16[8,2048,1408]{2,1,0:T(8,128)(2,1)} %refs_2_.3, f32[8256,128]{1,0:T(8,128)} %get-tuple-element.48.refs_3_), custom_call_target="tpu_custom_call" | custom-call | flops 35433480192 | bytes 92274688 | tf_op jit(solution)/shard_map/gate_up/pallas_call | solution.py:118
  286.4 1.6 collective-permute-start.5
  288.0 20.6 %down_combine.10 = (f32[8256,128]{1,0:T(8,128)}, f32[8256,128]{1,0:T(8,128)}) custom-call(s32[1]{0:T(128)} %bitcast.q_ref, s32[1]{0:T(128)} %bitcast.1.core_ref, s32[64]{0:T(128)} %reshape.31.n_ref, s32[4,8,1,384]{3,2,1,0:T(1,128)} %reshape.32.refs_0_.refs_1_, f32[4,8,1,384]{3,2,1,0:T(1,128)} %reshape.33.refs_1_.refs_2_.refs_3_, ...), custom_call_target="tpu_custom_call" | custom-call | flops 8858370048 | bytes 31522816 | tf_op jit(solution)/shard_map/down_combine/pallas_call | solution.py:219
  308.6 20.8 %down_combine.11 = (f32[8256,128]{1,0:T(8,128)}, f32[8256,128]{1,0:T(8,128)}) custom-call(s32[1]{0:T(128)} %bitcast.q_ref, s32[1]{0:T(128)} %bitcast.1.core_ref, s32[64]{0:T(128)} %reshape.31.n_ref, s32[4,8,1,384]{3,2,1,0:T(1,128)} %reshape.32.refs_0_.refs_1_, f32[4,8,1,384]{3,2,1,0:T(1,128)} %reshape.33.refs_1_.refs_2_.refs_3_, ...), custom_call_target="tpu_custom_call" | custom-call | flops 8858370048 | bytes 31522816 | tf_op jit(solution)/shard_map/down_combine/pallas_call | solution.py:219
  329.3 10.1 %collective-permute-start.7 = (f32[4096,128]{1,0:T(8,128)}, f32[4096,128]{1,0:T(8,128)S(1)}, u32[]{:S(2)}, u32[]{:S(2)}) collective-permute-start(f32[4096,128]{1,0:T(8,128)} %get-tuple-element.66.refs_5_), channel_id=1, source_target_pairs={{0,2},{1,3},{2,0},{3,1},{4,6},{5,7},{6,4},{7,5}} | collective-permute-start | bytes 6291464 | tf_op jit(solution)/shard_map/ppermute | solution.py:289
  339.5 4.5 add_add_fusion
  344.0 3.3 add_add_fusion.1
  347.3 2.4 slice_add_fusion.3
  349.8 31.4 %collective-permute-done.7 = f32[4096,128]{1,0:T(8,128)S(1)} collective-permute-done((f32[4096,128]{1,0:T(8,128)}, f32[4096,128]{1,0:T(8,128)S(1)}, u32[]{:S(2)}, u32[]{:S(2)}) %collective-permute-start.7) | collective-permute-done | bytes 2097184 | tf_op jit(solution)/shard_map/ppermute | solution.py:289
  381.2 6.3 %collective-permute-done.8 = f32[4096,128]{1,0:T(8,128)S(1)} collective-permute-done((f32[4096,128]{1,0:T(8,128)S(1)}, f32[4096,128]{1,0:T(8,128)S(1)}, u32[]{:S(2)}, u32[]{:S(2)}) %collective-permute-start.8) | collective-permute-done | bytes 2097184 | tf_op jit(solution)/shard_map/ppermute | solution.py:289
  387.9 2.0 collective-permute-start.13
  389.9 2.6 slice_add_fusion.1
  392.5 3.2 add_add_fusion.2
  395.7 3.2 slice_add_fusion.8
  398.9 1.7 collective-permute-start.15
  400.6 3.3 slice_add_fusion.6
  404.0 32.3 %collective-permute-done.19.b2_ref = f32[4096,128]{1,0:T(8,128)S(1)} collective-permute-done((f32[4096,128]{1,0:T(8,128)}, f32[4096,128]{1,0:T(8,128)S(1)}, u32[]{:S(2)}, u32[]{:S(2)}) %collective-permute-start.19) | collective-permute-done | bytes 2097184 | tf_op jit(solution)/shard_map/ppermute | solution.py:289
  436.6 3.2 add_add_fusion.3
  439.8 41.4 %collective-permute-done.13 = f32[4096,128]{1,0:T(8,128)S(1)} collective-permute-done((f32[4096,128]{1,0:T(8,128)S(1)}, f32[4096,128]{1,0:T(8,128)S(1)}, u32[]{:S(2)}, u32[]{:S(2)}) %collective-permute-start.13) | collective-permute-done | bytes 2097184 | tf_op jit(solution)/shard_map/ppermute | solution.py:289
  481.2 1.3 copy-done.2
  482.5 1.3 copy-done.3
  484.1 4.5 fusion.7
  488.6 3.9 final_sum.2.rest_0_
  492.4 33.8 %collective-permute-done.4 = f32[4096,128]{1,0:T(8,128)} collective-permute-done((f32[4096,128]{1,0:T(8,128)}, f32[4096,128]{1,0:T(8,128)}, u32[]{:S(2)}, u32[]{:S(2)}) %collective-permute-start.4) | collective-permute-done | bytes 2097184 | tf_op jit(solution)/shard_map/ppermute | solution.py:289
  526.3 3.2 fusion.9
  529.5 40.3 %collective-permute-done.10.b2_ref = f32[4096,128]{1,0:T(8,128)S(1)} collective-permute-done((f32[4096,128]{1,0:T(8,128)}, f32[4096,128]{1,0:T(8,128)S(1)}, u32[]{:S(2)}, u32[]{:S(2)}) %collective-permute-start.10) | collective-permute-done | bytes 2097184 | tf_op jit(solution)/shard_map/ppermute | solution.py:289
  569.7 3.8 final_sum.3
  (70 shorter events, 1.7 us)
Async XLA Ops:
  0.0 2.7 copy-start.4
  6.8 49.0 %all-to-all-start = ((f32[8,2,8,192]{3,2,1,0:T(8,128)}), f32[8,2,8,192]{3,2,1,0:T(8,128)S(1)}, u32[]{:S(2)}, u32[]{:S(2)}) async-start(f32[8,2,8,192]{3,2,1,0:T(8,128)} %copy.22), calls=%async_computation | async-start | bytes 262144 | tf_op jit(solution)/shard_map/all_to_all | solution.py:300
  81.0 24.8 %collective-permute-start = (f32[8256,128]{1,0:T(8,128)}, f32[8256,128]{1,0:T(8,128)}, u32[]{:S(2)}, u32[]{:S(2)}) collective-permute-start(f32[8256,128]{1,0:T(8,128)} %get-tuple-element.34), channel_id=1, source_target_pairs={{0,1},{1,0},{2,3},{3,2},{4,5},{5,4},{6,7},{7,6}} | collective-permute-start | bytes 12681224 | tf_op jit(solution)/shard_map/ppermute | solution.py:289
  104.6 9.9 %collective-permute-start.1 = (f32[8256,128]{1,0:T(8,128)}, f32[8256,128]{1,0:T(8,128)}, u32[]{:S(2)}, u32[]{:S(2)}) collective-permute-start(f32[8256,128]{1,0:T(8,128)} %get-tuple-element.36), channel_id=1, source_target_pairs={{0,1},{1,0},{2,3},{3,2},{4,5},{5,4},{6,7},{7,6}} | collective-permute-start | bytes 12681224 | tf_op jit(solution)/shard_map/ppermute | solution.py:289
  105.2 9.3 %slice-start.4 = ((s8[4227072]{0:T(1024)(128)(4,1)}), s8[4194304]{0:T(1024)(128)(4,1)S(1)}, s32[]{:S(2)}) async-start(s8[4227072]{0:T(1024)(128)(4,1)} %bitcast.37), calls=%async_computation.5 | async-start | bytes 8388608
  105.8 8.7 %slice-start.5 = ((s8[4227072]{0:T(1024)(128)(4,1)}), s8[32768]{0:T(1024)(128)(4,1)S(1)}, s32[]{:S(2)}) async-start(s8[4227072]{0:T(1024)(128)(4,1)} %bitcast.37), calls=%async_computation.6 | async-start | bytes 65536
  112.0 174.4 %collective-permute-start.16 = (f32[4096,128]{1,0:T(8,128)}, f32[4096,128]{1,0:T(8,128)}, u32[]{:S(2)}, u32[]{:S(2)}) collective-permute-start(f32[4096,128]{1,0:T(8,128)} %get-tuple-element.62.refs_4_), channel_id=1, source_target_pairs={{0,2},{1,3},{2,0},{3,1},{4,6},{5,7},{6,4},{7,5}} | collective-permute-start | bytes 6291464 | tf_op jit(solution)/shard_map/ppermute | solution.py:289
  207.7 131.7 %collective-permute-start.12 = (f32[8256,128]{1,0:T(8,128)}, f32[8256,128]{1,0:T(8,128)}, u32[]{:S(2)}, u32[]{:S(2)}) collective-permute-start(f32[8256,128]{1,0:T(8,128)} %get-tuple-element.52), channel_id=1, source_target_pairs={{0,1},{1,0},{2,3},{3,2},{4,5},{5,4},{6,7},{7,6}} | collective-permute-start | bytes 12681224 | tf_op jit(solution)/shard_map/ppermute | solution.py:289
  212.3 127.1 %collective-permute-start.14 = (f32[8256,128]{1,0:T(8,128)}, f32[8256,128]{1,0:T(8,128)}, u32[]{:S(2)}, u32[]{:S(2)}) collective-permute-start(f32[8256,128]{1,0:T(8,128)} %get-tuple-element.54), channel_id=1, source_target_pairs={{0,1},{1,0},{2,3},{3,2},{4,5},{5,4},{6,7},{7,6}} | collective-permute-start | bytes 12681224 | tf_op jit(solution)/shard_map/ppermute | solution.py:289
  212.4 117.0 %collective-permute-start.17 = (f32[4096,128]{1,0:T(8,128)}, f32[4096,128]{1,0:T(8,128)}, u32[]{:S(2)}, u32[]{:S(2)}) collective-permute-start(f32[4096,128]{1,0:T(8,128)} %get-tuple-element.61), channel_id=1, source_target_pairs={{0,4},{1,5},{2,6},{3,7},{4,0},{5,1},{6,2},{7,3}} | collective-permute-start | bytes 6291464 | tf_op jit(solution)/shard_map/ppermute | solution.py:289
  243.4 144.2 %collective-permute-start.3 = (f32[8256,128]{1,0:T(8,128)}, f32[8256,128]{1,0:T(8,128)}, u32[]{:S(2)}, u32[]{:S(2)}) collective-permute-start(f32[8256,128]{1,0:T(8,128)} %get-tuple-element.42), channel_id=1, source_target_pairs={{0,1},{1,0},{2,3},{3,2},{4,5},{5,4},{6,7},{7,6}} | collective-permute-start | bytes 12681224 | tf_op jit(solution)/shard_map/ppermute | solution.py:289
  286.4 101.5 %collective-permute-start.5 = (f32[8256,128]{1,0:T(8,128)}, f32[8256,128]{1,0:T(8,128)}, u32[]{:S(2)}, u32[]{:S(2)}) collective-permute-start(f32[8256,128]{1,0:T(8,128)} %get-tuple-element.44), channel_id=1, source_target_pairs={{0,1},{1,0},{2,3},{3,2},{4,5},{5,4},{6,7},{7,6}} | collective-permute-start | bytes 12681224 | tf_op jit(solution)/shard_map/ppermute | solution.py:289
  308.6 30.9 %copy-start.1 = (f32[4096,128]{1,0:T(8,128)S(1)}, f32[4096,128]{1,0:T(8,128)}, u32[]{:S(2)}) copy-start(f32[4096,128]{1,0:T(8,128)} %get-tuple-element.65) | copy-start | bytes 6291460
  329.3 51.8 %collective-permute-start.7 = (f32[4096,128]{1,0:T(8,128)}, f32[4096,128]{1,0:T(8,128)S(1)}, u32[]{:S(2)}, u32[]{:S(2)}) collective-permute-start(f32[4096,128]{1,0:T(8,128)} %get-tuple-element.66.refs_5_), channel_id=1, source_target_pairs={{0,2},{1,3},{2,0},{3,1},{4,6},{5,7},{6,4},{7,5}} | collective-permute-start | bytes 6291464 | tf_op jit(solution)/shard_map/ppermute | solution.py:289
  339.5 59.4 %collective-permute-start.11 = (f32[8256,128]{1,0:T(8,128)}, f32[8256,128]{1,0:T(8,128)S(1)}, u32[]{:S(2)}, u32[]{:S(2)}) collective-permute-start(f32[8256,128]{1,0:T(8,128)} %get-tuple-element.51), channel_id=1, source_target_pairs={{0,1},{1,0},{2,3},{3,2},{4,5},{5,4},{6,7},{7,6}} | collective-permute-start | bytes 12681224 | tf_op jit(solution)/shard_map/ppermute | solution.py:289
  339.5 48.0 %collective-permute-start.8 = (f32[4096,128]{1,0:T(8,128)S(1)}, f32[4096,128]{1,0:T(8,128)S(1)}, u32[]{:S(2)}, u32[]{:S(2)}) collective-permute-start(f32[4096,128]{1,0:T(8,128)S(1)} %copy-done.1), channel_id=1, source_target_pairs={{0,4},{1,5},{2,6},{3,7},{4,0},{5,1},{6,2},{7,3}} | collective-permute-start | bytes 6291464 | tf_op jit(solution)/shard_map/ppermute | solution.py:289
  344.0 48.4 %slice-start.2 = ((s8[4227072]{0:T(1024)(128)(4,1)}), s8[4194304]{0:T(1024)(128)(4,1)S(1)}, s32[]{:S(2)}) async-start(s8[4227072]{0:T(1024)(128)(4,1)} %bitcast.35), calls=%async_computation.3 | async-start | bytes 8388608
  347.3 45.1 %slice-start.3 = ((s8[4227072]{0:T(1024)(128)(4,1)}), s8[32768]{0:T(1024)(128)(4,1)S(1)}, s32[]{:S(2)}) async-start(s8[4227072]{0:T(1024)(128)(4,1)} %bitcast.35), calls=%async_computation.4 | async-start | bytes 65536
  381.2 111.2 %collective-permute-start.2 = (f32[8256,128]{1,0:T(8,128)}, f32[8256,128]{1,0:T(8,128)S(1)}, u32[]{:S(2)}, u32[]{:S(2)}) collective-permute-start(f32[8256,128]{1,0:T(8,128)} %get-tuple-element.41), channel_id=1, source_target_pairs={{0,1},{1,0},{2,3},{3,2},{4,5},{5,4},{6,7},{7,6}} | collective-permute-start | bytes 12681224 | tf_op jit(solution)/shard_map/ppermute | solution.py:289
  387.5 48.7 %collective-permute-start.19 = (f32[4096,128]{1,0:T(8,128)}, f32[4096,128]{1,0:T(8,128)S(1)}, u32[]{:S(2)}, u32[]{:S(2)}) collective-permute-start(f32[4096,128]{1,0:T(8,128)} %add_add_fusion), channel_id=1, source_target_pairs={{0,2},{1,3},{2,0},{3,1},{4,6},{5,7},{6,4},{7,5}} | collective-permute-start | bytes 6291464 | tf_op jit(solution)/shard_map/ppermute | solution.py:289
  387.6 48.7 %collective-permute-start.18 = (f32[4096,128]{1,0:T(8,128)S(1)}, f32[4096,128]{1,0:T(8,128)S(1)}, u32[]{:S(2)}, u32[]{:S(2)}) collective-permute-start(f32[4096,128]{1,0:T(8,128)S(1)} %add_add_fusion.1), channel_id=1, source_target_pairs={{0,4},{1,5},{2,6},{3,7},{4,0},{5,1},{6,2},{7,3}} | collective-permute-start | bytes 6291464 | tf_op jit(solution)/shard_map/ppermute | solution.py:289
  387.9 93.3 %collective-permute-start.13 = (f32[4096,128]{1,0:T(8,128)S(1)}, f32[4096,128]{1,0:T(8,128)S(1)}, u32[]{:S(2)}, u32[]{:S(2)}) collective-permute-start(f32[4096,128]{1,0:T(8,128)S(1)} %slice_add_fusion.3), channel_id=1, source_target_pairs={{0,2},{1,3},{2,0},{3,1},{4,6},{5,7},{6,4},{7,5}} | collective-permute-start | bytes 6291464 | tf_op jit(solution)/shard_map/ppermute | solution.py:289
  389.8 10.8 %slice-start.6 = ((s8[4227072]{0:T(1024)(128)(4,1)}), s8[4194304]{0:T(1024)(128)(4,1)S(1)}, s32[]{:S(2)}) async-start(s8[4227072]{0:T(1024)(128)(4,1)} %bitcast.39), calls=%async_computation.7 | async-start | bytes 8388608
  392.5 8.2 %slice-start.7 = ((s8[4227072]{0:T(1024)(128)(4,1)}), s8[32768]{0:T(1024)(128)(4,1)S(1)}, s32[]{:S(2)}) async-start(s8[4227072]{0:T(1024)(128)(4,1)} %bitcast.39), calls=%async_computation.8 | async-start | bytes 65536
  398.9 5.1 copy-start
  398.9 82.3 %collective-permute-start.15 = (f32[4096,128]{1,0:T(8,128)S(1)}, f32[4096,128]{1,0:T(8,128)S(1)}, u32[]{:S(2)}, u32[]{:S(2)}) collective-permute-start(f32[4096,128]{1,0:T(8,128)S(1)} %slice_add_fusion.1), channel_id=1, source_target_pairs={{0,4},{1,5},{2,6},{3,7},{4,0},{5,1},{6,2},{7,3}} | collective-permute-start | bytes 6291464 | tf_op jit(solution)/shard_map/ppermute | solution.py:289
  400.6 83.4 %slice-start = ((s8[4227072]{0:T(1024)(128)(4,1)}), s8[4194304]{0:T(1024)(128)(4,1)S(1)}, s32[]{:S(2)}) async-start(s8[4227072]{0:T(1024)(128)(4,1)} %bitcast.33), calls=%async_computation.1 | async-start | bytes 8388608
  404.0 80.1 %slice-start.1 = ((s8[4227072]{0:T(1024)(128)(4,1)}), s8[32768]{0:T(1024)(128)(4,1)S(1)}, s32[]{:S(2)}) async-start(s8[4227072]{0:T(1024)(128)(4,1)} %bitcast.33), calls=%async_computation.2 | async-start | bytes 65536
  436.2 90.0 %collective-permute-start.4 = (f32[4096,128]{1,0:T(8,128)}, f32[4096,128]{1,0:T(8,128)}, u32[]{:S(2)}, u32[]{:S(2)}) collective-permute-start(f32[4096,128]{1,0:T(8,128)} %slice_add_fusion.8), channel_id=1, source_target_pairs={{0,2},{1,3},{2,0},{3,1},{4,6},{5,7},{6,4},{7,5}} | collective-permute-start | bytes 6291464 | tf_op jit(solution)/shard_map/ppermute | solution.py:289
  436.3 89.9 %collective-permute-start.6 = (f32[4096,128]{1,0:T(8,128)}, f32[4096,128]{1,0:T(8,128)}, u32[]{:S(2)}, u32[]{:S(2)}) collective-permute-start(f32[4096,128]{1,0:T(8,128)} %slice_add_fusion.6), channel_id=1, source_target_pairs={{0,4},{1,5},{2,6},{3,7},{4,0},{5,1},{6,2},{7,3}} | collective-permute-start | bytes 6291464 | tf_op jit(solution)/shard_map/ppermute | solution.py:289
  481.2 1.3 copy-start.2
  481.2 88.5 %collective-permute-start.10 = (f32[4096,128]{1,0:T(8,128)}, f32[4096,128]{1,0:T(8,128)S(1)}, u32[]{:S(2)}, u32[]{:S(2)}) collective-permute-start(f32[4096,128]{1,0:T(8,128)} %add_add_fusion.2), channel_id=1, source_target_pairs={{0,2},{1,3},{2,0},{3,1},{4,6},{5,7},{6,4},{7,5}} | collective-permute-start | bytes 6291464 | tf_op jit(solution)/shard_map/ppermute | solution.py:289
  482.5 1.3 copy-start.3
  483.8 85.9 %collective-permute-start.9 = (f32[4096,128]{1,0:T(8,128)}, f32[4096,128]{1,0:T(8,128)S(1)}, u32[]{:S(2)}, u32[]{:S(2)}) collective-permute-start(f32[4096,128]{1,0:T(8,128)} %add_add_fusion.3), channel_id=1, source_target_pairs={{0,4},{1,5},{2,6},{3,7},{4,0},{5,1},{6,2},{7,3}} | collective-permute-start | bytes 6291464 | tf_op jit(solution)/shard_map/ppermute | solution.py:289
  488.6 37.7 %slice-start.8 = ((s8[4227072]{0:T(1024)(128)(4,1)}), s8[4194304]{0:T(1024)(128)(4,1)S(1)}, s32[]{:S(2)}) async-start(s8[4227072]{0:T(1024)(128)(4,1)} %bitcast.41), calls=%async_computation.9 | async-start | bytes 8388608
  488.6 37.7 %slice-start.9 = ((s8[4227072]{0:T(1024)(128)(4,1)}), s8[32768]{0:T(1024)(128)(4,1)S(1)}, s32[]{:S(2)}) async-start(s8[4227072]{0:T(1024)(128)(4,1)} %bitcast.41), calls=%async_computation.10 | async-start | bytes 65536

commit v2 on v0

v2 whole, which is shorter than its diff:
```python
import jax
import jax.numpy as jnp
from jax import lax
from jax.experimental import pallas as pl
from jax.experimental.pallas import tpu as pltpu
from jax.sharding import PartitionSpec as P


GROUP_AXES = ('eo', 'em', 'ei')
LANES = 128
COLS = 1024
JT = COLS // LANES
ANY = pl.ANY


def slot_tables(slot_idx, expert_idx, gate_wt, n_exp, n_slot):
    n_tok, top = slot_idx.shape
    tok = lax.broadcasted_iota(jnp.int32, (n_tok, top), 0)
    spare = float(n_tok * JT)
    delta = (tok * JT).astype(jnp.float32) - spare
    exp_hot = (expert_idx[:, :, None] == lax.broadcasted_iota(jnp.int32, (1, 1, n_exp), 2)).astype(jnp.float32)
    slot_hot = (slot_idx[:, :, None] == lax.broadcasted_iota(jnp.int32, (1, 1, n_slot), 2)).astype(jnp.float32)
    both = jnp.concatenate([exp_hot * delta[:, :, None], exp_hot * gate_wt[:, :, None]], axis=2)
    table = jnp.einsum('tje,tjc->ec', both, slot_hot, precision=lax.Precision.HIGHEST,
                       preferred_element_type=jnp.float32)
    addr, wt = table[:n_exp] + spare, table[n_exp:]
    return jnp.stack([addr, wt])


def round16(n):
    return (n + 15) // 16 * 16


def row_chunks(total, body):
    whole = (total + 127) // 256
    rest = total - whole * 256

    def chunk(c, carry):
        body(pl.multiple_of(c * 256, 256), 256)
        return carry

    lax.fori_loop(0, whole, chunk, 0)
    pl.when(rest > 0)(lambda: body(pl.multiple_of(whole * 256, 256), 128))


def gate_up_tile(x, wg_ref, wu_ref, cols):
    w = jnp.concatenate([wg_ref[:, cols], wu_ref[:, cols]], axis=1)
    gu = jnp.dot(x, w, preferred_element_type=jnp.float32)
    g, u = gu[:, :LANES], gu[:, LANES:]
    return ((g * jax.nn.sigmoid(g)) * u).astype(jnp.bfloat16)


def pass_kernel(src_ref, core_ref, n_ref, *refs):
    x_refs, addr_refs, wt_refs, weights = refs[0:2], refs[2:4], refs[4:6], refs[6:9]
    outs, bufs, (h_ref, xs_ref, y_ref, acc_ref, w_sem, sem) = refs[-13:-9], refs[-9:-6], refs[-6:]
    ff = h_ref.shape[1]
    e = pl.program_id(0)
    n_exp = pl.num_programs(0)
    slot = e % 2

    def fetch(k, expert, into):
        return pltpu.make_async_copy(weights[k].at[expert], bufs[k].at[into], w_sem.at[into, k])

    @pl.when(e == 0)
    def _():
        for k in range(3):
            fetch(k, 0, 0).start()

    @pl.when(e + 1 < n_exp)
    def _():
        for k in range(3):
            fetch(k, e + 1, 1 - slot).start()

    @pl.when(e == 0)
    def _():
        def zero(i, carry):
            r = pl.ds(pl.multiple_of(i * 8 * JT, 8 * JT), 8 * JT)
            for k in range(acc_ref.shape[0]):
                acc_ref[k, r, :] = jnp.zeros((8 * JT, LANES), jnp.float32)
            return carry

        lax.fori_loop(0, acc_ref.shape[1] // (8 * JT), zero, 0)

    counts = [n_ref[src_ref[i] * n_exp + e] for i in range(2)]
    first = [jnp.int32(0), round16(counts[0])]
    total = first[1] + round16(counts[1])

    for i in range(2):
        def copy(b, carry):
            xs_ref[pl.ds(pl.multiple_of(first[i] + b * 16, 16), 16), :] = (
                x_refs[i][0, 0, pl.ds(pl.multiple_of(b * 16, 16), 16), :])
            return carry

        lax.fori_loop(0, round16(counts[i]) // 16, copy, 0)

    fetch(0, e, slot).wait()
    fetch(1, e, slot).wait()
    wg_ref, wu_ref, wd_ref = (buf.at[slot] for buf in bufs)

    def hidden(r0, rows):
        r = pl.ds(r0, rows)
        for j in range(ff // LANES):
            cols = slice(j * LANES, (j + 1) * LANES)
            h_ref[r, cols] = gate_up_tile(xs_ref[r, :], wg_ref, wu_ref, cols)

    row_chunks(total, hidden)
    fetch(2, e, slot).wait()

    def result(r0, rows):
        for jj in range(wd_ref.shape[1] // 256):
            y = jnp.dot(h_ref[pl.ds(r0, rows), :], wd_ref[:, jj * 256:(jj + 1) * 256],
                        preferred_element_type=jnp.float32)
            y = y.astype(jnp.bfloat16).astype(jnp.float32)
            for k in range(2):
                y_ref[pl.ds(r0 // 8, rows // 8), (jj * 2 + k) * 8:(jj * 2 + k + 1) * 8, :] = (
                    y[:, k * LANES:(k + 1) * LANES].reshape(rows // 8, 8, LANES))

    row_chunks(total, result)

    for i in range(2):
        y0 = first[i] // 8

        def batch(b, carry):
            at = [pl.ds(pl.multiple_of(addr_refs[i][0, 0, 0, b * 8 + k], JT), JT) for k in range(8)]
            wts = [wt_refs[i][0, 0, 0, b * 8 + k] for k in range(8)]
            work = [(k, col) for k in range(8) for col in range(2)]
            ys = [y_ref[y0 + b, pl.ds(col * 8 * JT + k, JT, stride=8), :] for k, col in work]
            old = [acc_ref[col * 2 + i, at[k], :] for k, col in work]
            for (k, col), y, a in zip(work, ys, old):
                acc_ref[col * 2 + i, at[k], :] = a + wts[k] * y
            return carry

        lax.fori_loop(0, (counts[i] + 7) // 8, batch, 0)

    @pl.when(e == n_exp - 1)
    def _():
        copies = []
        for col in range(2):
            for i in range(2):
                own = core_ref[0] == i
                k = col * 2 + i
                for dst, cond in ((outs[col * 2], own), (outs[col * 2 + 1], jnp.logical_not(own))):
                    copies.append((cond, pltpu.make_async_copy(acc_ref.at[k], dst, sem.at[k])))
        for cond, copy in copies:
            pl.when(cond)(copy.start)
        for cond, copy in copies:
            pl.when(cond)(copy.wait)


def ffn_pass(src, core, count, addr, wt, x, wg, wu, wd, n_tok, after):
    _, n_exp, slots, width = x.shape
    ff = wg.shape[2]
    rows = 2 * slots
    acc_rows = (n_tok + 8) * JT
    acc = jax.ShapeDtypeStruct((acc_rows, LANES), jnp.float32)
    x_specs = [pl.BlockSpec((1, 1, slots, width), lambda e, src, *_, i=i: (src[i], e, 0, 0)) for i in range(2)]
    table_specs = [pl.BlockSpec((1, 1, 1, slots), lambda e, src, *_, i=i: (src[i], e, 0, 0),
                                memory_space=pltpu.SMEM) for i in range(2)]
    return pl.pallas_call(
        pass_kernel,
        grid_spec=pltpu.PrefetchScalarGridSpec(
            num_scalar_prefetch=3, grid=(n_exp,),
            in_specs=x_specs + table_specs * 2 + [pl.BlockSpec(memory_space=ANY)] * (3 + len(after)),
            out_specs=[pl.BlockSpec(memory_space=ANY)] * 4,
            scratch_shapes=[pltpu.VMEM((2,) + w.shape[1:], jnp.bfloat16) for w in (wg, wu, wd)] +
                           [pltpu.VMEM((rows, ff), jnp.bfloat16),
                            pltpu.VMEM((rows, width), jnp.bfloat16),
                            pltpu.VMEM((rows // 8, 8 * width // LANES, LANES), jnp.float32),
                            pltpu.VMEM((4, acc_rows, LANES), jnp.float32),
                            pltpu.SemaphoreType.DMA((2, 3)),
                            pltpu.SemaphoreType.DMA((4,))]),
        out_shape=[acc] * 4,
        compiler_params=pltpu.CompilerParams(dimension_semantics=('arbitrary',), vmem_limit_bytes=67043328),
        cost_estimate=pl.CostEstimate(flops=2 * n_exp * rows * width * ff * 3, transcendentals=0,
                                      bytes_accessed=3 * n_exp * width * ff * 2),
        name='ffn_pass',
    )(src, core, count, x, x, addr, addr, wt, wt, wg, wu, wd, *after)


def final_kernel(a1_ref, a2_ref, b1_ref, b2_ref, *rest):
    out_ref, s_ref = rest[-2:]
    step = pl.program_id(0)
    half = pl.num_programs(0) // 2

    def emit(a_ref, b_ref):
        def body(b, carry):
            r = pl.ds(pl.multiple_of(b * 16 * JT, 16 * JT), 16 * JT)
            s_ref[r, :] = a_ref[r, :] + b_ref[r, :]
            for j in range(JT):
                pair = [s_ref[pl.ds((b * 16 + k) * JT + j, 8, stride=JT), :] for k in (0, 8)]
                out_ref[pl.ds(pl.multiple_of(b * 16, 16), 16), j * LANES:(j + 1) * LANES] = (
                    jnp.concatenate(pair, axis=0).astype(out_ref.dtype))
            return carry

        lax.fori_loop(0, out_ref.shape[0] // 16, body, 0)

    pl.when(step < half)(lambda: emit(a1_ref, b1_ref))
    pl.when(step >= half)(lambda: emit(a2_ref, b2_ref))


def final_sum(a1, a2, b1, b2, n, n_tok, width, out):
    tb = 128
    steps = n_tok // tb
    half = steps // 2
    low = pl.BlockSpec((tb * JT, LANES), lambda i: (jnp.minimum(i, half - 1), 0))
    high = pl.BlockSpec((tb * JT, LANES), lambda i: (jnp.maximum(i - half, 0), 0))
    prior = [] if out is None else [out]
    return pl.pallas_call(
        final_kernel,
        grid=(steps,),
        in_specs=[low, high, low, high] + [pl.BlockSpec(memory_space=ANY)] * len(prior),
        out_specs=pl.BlockSpec((tb, COLS), lambda i: (i, n)),
        scratch_shapes=[pltpu.VMEM((tb * JT, LANES), jnp.float32)],
        out_shape=jax.ShapeDtypeStruct((n_tok, width), jnp.bfloat16),
        input_output_aliases={4: 0} if prior else {},
        compiler_params=pltpu.CompilerParams(dimension_semantics=('arbitrary',), vmem_limit_bytes=30 * 2 ** 20),
        cost_estimate=pl.CostEstimate(flops=10 ** 7, transcendentals=0, bytes_accessed=n_tok * COLS * 10),
        name='final_sum',
    )(a1, a2, b1, b2, *prior)


def solution(mesh):
    token_spec = P(('dp',) + GROUP_AXES, None)
    weight_spec = P(GROUP_AXES, None, None)
    rows_spec = P('dp', GROUP_AXES, None, None)
    n_dev = mesh.shape['eo'] * mesh.shape['em'] * mesh.shape['ei']
    core_bit, x_bit, y_bit = 1, 2, 4
    to_pair = [(i, i ^ core_bit) for i in range(n_dev)]
    straight = [(i, i ^ (y_bit if i & core_bit else x_bit)) for i in range(n_dev)]
    crossed = [(i, i ^ (x_bit if i & core_bit else y_bit)) for i in range(n_dev)]

    def send(a, pairs):
        return lax.ppermute(a, GROUP_AXES, pairs)

    def local_part(x_local, w_gate, w_up, w_down, slot_idx, expert_idx, gate_wt):
        _, n_exp, slots, width = x_local.shape
        n_tok = slot_idx.shape[0]
        core = lax.axis_index('ei').astype(jnp.int32).reshape(1)
        chip = (lax.axis_index('eo') * 2 + lax.axis_index('em')).astype(jnp.int32)

        table = slot_tables(slot_idx, expert_idx, gate_wt, n_dev * n_exp, slots)
        table = table.reshape(2, n_dev, n_exp, slots).swapaxes(0, 1)
        table = lax.all_to_all(table, GROUP_AXES, 0, 0, tiled=True)
        addr = table[:, 0].astype(jnp.int32)
        wt = table[:, 1]
        seen = jnp.where(wt > 0, lax.broadcasted_iota(jnp.int32, wt.shape, 2) + 1, 0)
        count = jnp.max(seen, axis=2).reshape(-1)
        addr, wt = addr[:, :, None], wt[:, :, None]

        lo, hi = slice(0, n_tok // 2 * JT), slice(n_tok // 2 * JT, n_tok * JT)
        blocks = range(width // COLS)

        def ffn(flips, after):
            src = jnp.stack([2 * (chip ^ f) + i for i, f in enumerate(flips)])
            own0, sib0, own1, sib1 = ffn_pass(src, core, count, addr, wt, x_local, w_gate, w_up, w_down, n_tok, after)
            return [(own0, send(sib0, to_pair)), (own1, send(sib1, to_pair))]

        relay_lo, relay_hi, gate = [], [], []
        for n, (own, sib) in zip(blocks, ffn((3, 3), [])):
            low, high = own[lo] + sib[lo], own[hi] + sib[hi]
            relay_lo.append(send(low, straight))
            relay_hi.append(send(high, crossed))
            gate.append(low)

        got, got2, after2 = [], [], []
        for n, (own, sib) in zip(blocks, ffn((1, 2), gate)):
            low = own[lo] + sib[lo]
            own, sib, relayed = lax.optimization_barrier((own, sib, relay_hi[n]))
            got.append((send(low, straight),
                        send(own[hi] + sib[hi] + relayed, straight)))
            after2.append(low)
        for n, (own, sib) in zip(blocks, ffn((2, 1), after2)):
            high = own[hi] + sib[hi]
            own, sib, relayed = lax.optimization_barrier((own, sib, relay_lo[n]))
            got2.append((send(own[lo] + sib[lo] + relayed, crossed),
                         send(high, crossed)))
            gate = [high]

        out = None
        for n, (own, sib) in zip(blocks, ffn((0, 0), gate)):
            out = final_sum(own[lo] + sib[lo] + got[n][0], own[hi] + sib[hi] + got[n][1],
                            got2[n][0], got2[n][1], n, n_tok, width, out)
        return out

    return jax.shard_map(local_part, mesh=mesh,
                         in_specs=(rows_spec, weight_spec, weight_spec, weight_spec, token_spec, token_spec, token_spec),
                         out_specs=token_spec, check_vma=False)
```

time: 1140 us -> 551 us (0.48)
  waiting for transfers between devices: 544 us -> 213 us
  local copies, waits for them, and re-layouts: 273 us -> 1.08 us
  matrix products: 274 us -> 3.18 us
  Pallas kernels: 0 us -> 253 us
  other arithmetic: 39 us -> 56.6 us
  starting transfers between devices: 7.61 us -> 23.7 us
    all_to_all x1, waiting for transfers between devices: 544 us -> 4.86 us  [local_part(): table = lax.all_to_all(table, GROUP_AXES, 0, 0, tiled=True)]
    dot_general x3 -> x1, matrix products: 274 us -> 3.18 us  [slot_tables(): jnp.einsum('tje,tjc->ec', both, slot_hot, precision=lax.Precision.HIGHEST...]
    pallas_call x0 -> x6, Pallas kernels: none -> 253 us  [the longest x4 245 us: ffn_pass(): pl.pallas_call(pass_kernel, grid_spec=pltpu.PrefetchScalarGridSpec(num_sc...]
    gather x2 -> x0, local copies, waits for them, and re-layouts: 238 us -> none  [combine_rows(): picked = jnp.take(flat_rows, row_index, axis=0)]
    ppermute x0 -> x20, waiting for transfers between devices: none -> 208 us  [send(): return lax.ppermute(a, GROUP_AXES, pairs)]
    add x0 -> x14, other arithmetic: none -> 49.5 us  [the longest x2 10.7 us: local_part(): low, high = (own[lo] + sib[lo], own[hi] + sib[hi])]
    reduce_sum x1 -> x0, other arithmetic: 39 us -> none  [combine_rows(): combined = jnp.sum(weight[:, :, None] * picked.astype(jnp.float32), axis=1)]
    convert_element_type x1 -> x0, local copies, waits for them, and re-layouts: 33.5 us -> none  [local_part(): jnp.einsum('escf,efd->escd', hidden, w_down, preferred_element_type=jnp.f...]
  transfers between devices with their start and end apart: 1 -> 21, of which waited for: 1 -> 12; matrix products, arithmetic and copies ran while one was open for 0% -> 8% of each run, Pallas kernels for 0% -> 12%
where the time goes in v2:
time: 551 us; the launch traced here: 550 us
  Pallas kernels  253 us (46%)
  waiting for transfers between devices  213 us (39%)
  other arithmetic  56.6 us (10%)
  starting transfers between devices  23.7 us (4%)
    pallas_call x4, Pallas kernels, ffn_pass(): pl.pallas_call(pass_kernel, grid_spec=pltpu.PrefetchScalarGridSpec(num_sc...  245 us
    ppermute x20, waiting for transfers between devices, send(): return lax.ppermute(a, GROUP_AXES, pairs)  208 us
    ppermute x20, starting transfers between devices, send(): return lax.ppermute(a, GROUP_AXES, pairs)  19.4 us
  transfers between devices with their start and end apart: 21, of which 12 were waited for; matrix products, arithmetic and copies ran while one was open for 8% of the time, Pallas kernels for 12%

profile of v2, /device:TPU:0, one launch (start us, length us, event | category | flops | bytes accessed | tf_op | source)
XLA Modules:
  0.0 550.5 jit_solution(2541903564548604721)
XLA Ops:
  0.0 2.7 fusion.5
  2.7 3.2 fusion.11
  6.3 0.8 maximum_bitcast_fusion
  7.1 4.3 all-to-all-start
  11.4 0.6 pad_add_fusion.3.src_ref
  12.0 4.9 all-to-all-done
  17.2 0.6 reshape.33.n_ref
  17.9 0.7 slice_bitcast_fusion
  18.6 61.3 %ffn_pass.4 = (f32[8256,128]{1,0:T(8,128)}, f32[8256,128]{1,0:T(8,128)}, f32[8256,128]{1,0:T(8,128)}, f32[8256,128]{1,0:T(8,128)}) custom-call(s32[2]{0:T(128)} %pad_add_fusion.3.src_ref, s32[1]{0:T(128)} %bitcast.2.core_ref, s32[64]{0:T(128)} %reshape.33.n_ref, bf16[8,8,192,2048]{3,2,1,0:T(8,128)(2,1)} %refs_1_.7, bf16[8,8,192,2048]{3,2,1,0:T(8,128)(2,1)} %refs_1_.7, ...), custom_call_target="tpu_custom_call" | custom-call | flops 53150220288 | bytes 138412032 | tf_op jit(solution)/shard_map/ffn_pass/pallas_call | solution.py:159
  79.9 1.8 collective-permute-start
  81.8 0.7 pad_add_fusion.2.src_ref
  82.4 6.5 %collective-permute-done = f32[8256,128]{1,0:T(8,128)} collective-permute-done((f32[8256,128]{1,0:T(8,128)}, f32[8256,128]{1,0:T(8,128)}, u32[]{:S(2)}, u32[]{:S(2)}) %collective-permute-start) | collective-permute-done | bytes 4227104 | tf_op jit(solution)/shard_map/ppermute | solution.py:233
  88.9 6.0 %slice_add_fusion.1 = (f32[4096,128]{1,0:T(8,128)}, f32[4096,128]{1,0:T(8,128)}) fusion(f32[8256,128]{1,0:T(8,128)} %collective-permute-done, f32[8256,128]{1,0:T(8,128)} %get-tuple-element.33), kind=kLoop, calls=%fused_computation.10 | loop fusion | flops 1048576 | bytes 12582912 | tf_op jit(solution)/shard_map/add | solution.py:260
  94.9 4.7 slice_add_fusion.4
  99.7 61.3 %ffn_pass.5 = (f32[8256,128]{1,0:T(8,128)}, f32[8256,128]{1,0:T(8,128)}, f32[8256,128]{1,0:T(8,128)}, f32[8256,128]{1,0:T(8,128)}) custom-call(s32[2]{0:T(128)} %pad_add_fusion.2.src_ref, s32[1]{0:T(128)} %bitcast.2.core_ref, s32[64]{0:T(128)} %reshape.33.n_ref, bf16[8,8,192,2048]{3,2,1,0:T(8,128)(2,1)} %refs_1_.7, bf16[8,8,192,2048]{3,2,1,0:T(8,128)(2,1)} %refs_1_.7, ...), custom_call_target="tpu_custom_call" | custom-call | flops 53150220288 | bytes 138412032 | tf_op jit(solution)/shard_map/ffn_pass/pallas_call | solution.py:159
  161.0 2.8 collective-permute-start.2
  163.8 0.7 pad_add_fusion.1.src_ref
  164.4 6.5 %collective-permute-done.2 = f32[8256,128]{1,0:T(8,128)} collective-permute-done((f32[8256,128]{1,0:T(8,128)}, f32[8256,128]{1,0:T(8,128)}, u32[]{:S(2)}, u32[]{:S(2)}) %collective-permute-start.2) | collective-permute-done | bytes 4227104 | tf_op jit(solution)/shard_map/ppermute | solution.py:233
  170.9 3.7 slice_add_fusion.9.refs_9_
  174.6 2.3 collective-permute-done.3
  176.9 3.8 slice_add_fusion.8.refs_10_
  180.7 61.5 %ffn_pass.6 = (f32[8256,128]{1,0:T(8,128)}, f32[8256,128]{1,0:T(8,128)}, f32[8256,128]{1,0:T(8,128)}, f32[8256,128]{1,0:T(8,128)}) custom-call(s32[2]{0:T(128)} %pad_add_fusion.1.src_ref, s32[1]{0:T(128)} %bitcast.2.core_ref, s32[64]{0:T(128)} %reshape.33.n_ref, bf16[8,8,192,2048]{3,2,1,0:T(8,128)(2,1)} %refs_1_.7, bf16[8,8,192,2048]{3,2,1,0:T(8,128)(2,1)} %refs_1_.7, ...), custom_call_target="tpu_custom_call" | custom-call | flops 53150220288 | bytes 138412032 | tf_op jit(solution)/shard_map/ffn_pass/pallas_call | solution.py:159
  242.3 2.7 collective-permute-start.4
  245.0 2.0 collective-permute-start.7
  247.6 2.0 collective-permute-start.9
  249.6 42.9 %collective-permute-done.14 = f32[4096,128]{1,0:T(8,128)S(1)} collective-permute-done((f32[4096,128]{1,0:T(8,128)}, f32[4096,128]{1,0:T(8,128)S(1)}, u32[]{:S(2)}, u32[]{:S(2)}) %collective-permute-start.14) | collective-permute-done | bytes 2097184 | tf_op jit(solution)/shard_map/ppermute | solution.py:233
  292.5 3.9 add_add_fusion.1
  296.4 41.2 %collective-permute-done.7 = f32[4096,128]{1,0:T(8,128)} collective-permute-done((f32[4096,128]{1,0:T(8,128)}, f32[4096,128]{1,0:T(8,128)}, u32[]{:S(2)}, u32[]{:S(2)}) %collective-permute-start.7) | collective-permute-done | bytes 2097184 | tf_op jit(solution)/shard_map/ppermute | solution.py:233
  337.6 3.8 slice_add_fusion.7.refs_9_
  341.3 61.4 %ffn_pass.7 = (f32[8256,128]{1,0:T(8,128)}, f32[8256,128]{1,0:T(8,128)}, f32[8256,128]{1,0:T(8,128)}, f32[8256,128]{1,0:T(8,128)}) custom-call(s32[2]{0:T(128)} %pad_add_fusion.src_ref, s32[1]{0:T(128)} %bitcast.2.core_ref, s32[64]{0:T(128)} %reshape.33.n_ref, bf16[8,8,192,2048]{3,2,1,0:T(8,128)(2,1)} %refs_1_.7, bf16[8,8,192,2048]{3,2,1,0:T(8,128)(2,1)} %refs_1_.7, ...), custom_call_target="tpu_custom_call" | custom-call | flops 53150220288 | bytes 138412032 | tf_op jit(solution)/shard_map/ffn_pass/pallas_call | solution.py:159
  402.7 3.1 collective-permute-start.12
  405.8 2.4 slice_add_fusion
  408.3 0.8 collective-permute-start.5
  409.1 3.3 add_add_fusion
  412.4 1.2 collective-permute-start.18
  413.7 4.5 add_add_fusion.3
  418.1 0.7 collective-permute-start.6
  418.8 29.6 %collective-permute-done.19.b2_ref = f32[4096,128]{1,0:T(8,128)S(1)} collective-permute-done((f32[4096,128]{1,0:T(8,128)S(1)}, f32[4096,128]{1,0:T(8,128)S(1)}, u32[]{:S(2)}, u32[]{:S(2)}) %collective-permute-start.19) | collective-permute-done | bytes 2097184 | tf_op jit(solution)/shard_map/ppermute | solution.py:233
  448.5 4.5 add_add_fusion.2
  453.0 40.3 %collective-permute-done.18.b1_ref = f32[4096,128]{1,0:T(8,128)S(1)} collective-permute-done((f32[4096,128]{1,0:T(8,128)S(1)}, f32[4096,128]{1,0:T(8,128)S(1)}, u32[]{:S(2)}, u32[]{:S(2)}) %collective-permute-start.18) | collective-permute-done | bytes 2097184 | tf_op jit(solution)/shard_map/ppermute | solution.py:233
  493.3 2.0 collective-permute-start.10
  495.4 4.5 fusion.7
  499.8 3.9 final_sum.2.rest_0_
  503.7 5.2 collective-permute-done.8
  508.9 4.5 fusion.9
  513.4 10.8 %collective-permute-done.11.b2_ref = f32[4096,128]{1,0:T(8,128)S(1)} collective-permute-done((f32[4096,128]{1,0:T(8,128)S(1)}, f32[4096,128]{1,0:T(8,128)S(1)}, u32[]{:S(2)}, u32[]{:S(2)}) %collective-permute-start.11) | collective-permute-done | bytes 2097184 | tf_op jit(solution)/shard_map/ppermute | solution.py:233
  524.2 22.5 %collective-permute-done.10.b1_ref = f32[4096,128]{1,0:T(8,128)S(1)} collective-permute-done((f32[4096,128]{1,0:T(8,128)}, f32[4096,128]{1,0:T(8,128)S(1)}, u32[]{:S(2)}, u32[]{:S(2)}) %collective-permute-start.10) | collective-permute-done | bytes 2097184 | tf_op jit(solution)/shard_map/ppermute | solution.py:233
  546.6 3.8 final_sum.3
  (52 shorter events, 1.7 us)
Async XLA Ops:
  0.0 2.7 copy-start.2
  7.1 9.8 %all-to-all-start = ((f32[8,2,8,192]{3,1,2,0:T(2,128)}), f32[8,2,8,192]{3,1,2,0:T(2,128)S(1)}, u32[]{:S(2)}, u32[]{:S(2)}) async-start(f32[8,2,8,192]{3,1,2,0:T(2,128)} %maximum_bitcast_fusion), calls=%async_computation | async-start | bytes 262144 | tf_op jit(solution)/shard_map/all_to_all | solution.py:243
  79.9 9.0 %collective-permute-start = (f32[8256,128]{1,0:T(8,128)}, f32[8256,128]{1,0:T(8,128)}, u32[]{:S(2)}, u32[]{:S(2)}) collective-permute-start(f32[8256,128]{1,0:T(8,128)} %get-tuple-element.34), channel_id=1, source_target_pairs={{0,1},{1,0},{2,3},{3,2},{4,5},{5,4},{6,7},{7,6}} | collective-permute-start | bytes 12681224 | tf_op jit(solution)/shard_map/ppermute | solution.py:233
  81.7 13.2 %collective-permute-start.1 = (f32[8256,128]{1,0:T(8,128)}, f32[8256,128]{1,0:T(8,128)}, u32[]{:S(2)}, u32[]{:S(2)}) collective-permute-start(f32[8256,128]{1,0:T(8,128)} %get-tuple-element.36), channel_id=1, source_target_pairs={{0,1},{1,0},{2,3},{3,2},{4,5},{5,4},{6,7},{7,6}} | collective-permute-start | bytes 12681224 | tf_op jit(solution)/shard_map/ppermute | solution.py:233
  88.9 6.0 %slice-start = ((s8[4227072]{0:T(1024)(128)(4,1)}), s8[4194304]{0:T(1024)(128)(4,1)S(1)}, s32[]{:S(2)}) async-start(s8[4227072]{0:T(1024)(128)(4,1)} %bitcast.19), calls=%async_computation.1 | async-start | bytes 8388608
  88.9 6.0 %slice-start.1 = ((s8[4227072]{0:T(1024)(128)(4,1)}), s8[32768]{0:T(1024)(128)(4,1)S(1)}, s32[]{:S(2)}) async-start(s8[4227072]{0:T(1024)(128)(4,1)} %bitcast.19), calls=%async_computation.2 | async-start | bytes 65536
  161.0 9.9 %collective-permute-start.2 = (f32[8256,128]{1,0:T(8,128)}, f32[8256,128]{1,0:T(8,128)}, u32[]{:S(2)}, u32[]{:S(2)}) collective-permute-start(f32[8256,128]{1,0:T(8,128)} %get-tuple-element.38), channel_id=1, source_target_pairs={{0,1},{1,0},{2,3},{3,2},{4,5},{5,4},{6,7},{7,6}} | collective-permute-start | bytes 12681224 | tf_op jit(solution)/shard_map/ppermute | solution.py:233
  163.7 13.2 %collective-permute-start.3 = (f32[8256,128]{1,0:T(8,128)}, f32[8256,128]{1,0:T(8,128)}, u32[]{:S(2)}, u32[]{:S(2)}) collective-permute-start(f32[8256,128]{1,0:T(8,128)} %get-tuple-element.40), channel_id=1, source_target_pairs={{0,1},{1,0},{2,3},{3,2},{4,5},{5,4},{6,7},{7,6}} | collective-permute-start | bytes 12681224 | tf_op jit(solution)/shard_map/ppermute | solution.py:233
  242.3 95.3 %collective-permute-start.4 = (f32[8256,128]{1,0:T(8,128)}, f32[8256,128]{1,0:T(8,128)}, u32[]{:S(2)}, u32[]{:S(2)}) collective-permute-start(f32[8256,128]{1,0:T(8,128)} %get-tuple-element.42), channel_id=1, source_target_pairs={{0,1},{1,0},{2,3},{3,2},{4,5},{5,4},{6,7},{7,6}} | collective-permute-start | bytes 12681224 | tf_op jit(solution)/shard_map/ppermute | solution.py:233
  245.0 47.6 %collective-permute-start.14 = (f32[4096,128]{1,0:T(8,128)}, f32[4096,128]{1,0:T(8,128)S(1)}, u32[]{:S(2)}, u32[]{:S(2)}) collective-permute-start(f32[4096,128]{1,0:T(8,128)} %get-tuple-element.63), channel_id=1, source_target_pairs={{0,4},{1,3},{2,6},{3,1},{4,0},{5,7},{6,2},{7,5}} | collective-permute-start | bytes 6291464 | tf_op jit(solution)/shard_map/ppermute | solution.py:233
  245.0 92.6 %collective-permute-start.7 = (f32[4096,128]{1,0:T(8,128)}, f32[4096,128]{1,0:T(8,128)}, u32[]{:S(2)}, u32[]{:S(2)}) collective-permute-start(f32[4096,128]{1,0:T(8,128)} %get-tuple-element.67), channel_id=1, source_target_pairs={{0,4},{1,3},{2,6},{3,1},{4,0},{5,7},{6,2},{7,5}} | collective-permute-start | bytes 6291464 | tf_op jit(solution)/shard_map/ppermute | solution.py:233
  247.6 155.1 %collective-permute-start.17 = (f32[4096,128]{1,0:T(8,128)}, f32[4096,128]{1,0:T(8,128)}, u32[]{:S(2)}, u32[]{:S(2)}) collective-permute-start(f32[4096,128]{1,0:T(8,128)} %get-tuple-element.64.refs_9_), channel_id=1, source_target_pairs={{0,2},{1,5},{2,0},{3,7},{4,6},{5,1},{6,4},{7,3}} | collective-permute-start | bytes 6291464 | tf_op jit(solution)/shard_map/ppermute | solution.py:233
  247.6 160.7 %collective-permute-start.9 = (f32[4096,128]{1,0:T(8,128)}, f32[4096,128]{1,0:T(8,128)}, u32[]{:S(2)}, u32[]{:S(2)}) collective-permute-start(f32[4096,128]{1,0:T(8,128)} %get-tuple-element.68.refs_10_), channel_id=1, source_target_pairs={{0,2},{1,5},{2,0},{3,7},{4,6},{5,1},{6,4},{7,3}} | collective-permute-start | bytes 6291464 | tf_op jit(solution)/shard_map/ppermute | solution.py:233
  292.5 119.9 %collective-permute-start.13 = (f32[4096,128]{1,0:T(8,128)}, f32[4096,128]{1,0:T(8,128)}, u32[]{:S(2)}, u32[]{:S(2)}) collective-permute-start(f32[4096,128]{1,0:T(8,128)} %slice_add_fusion.9.refs_9_), channel_id=1, source_target_pairs={{0,2},{1,5},{2,0},{3,7},{4,6},{5,1},{6,4},{7,3}} | collective-permute-start | bytes 6291464 | tf_op jit(solution)/shard_map/ppermute | solution.py:233
  337.6 80.6 %collective-permute-start.15 = (f32[4096,128]{1,0:T(8,128)}, f32[4096,128]{1,0:T(8,128)}, u32[]{:S(2)}, u32[]{:S(2)}) collective-permute-start(f32[4096,128]{1,0:T(8,128)} %add_add_fusion.1), channel_id=1, source_target_pairs={{0,2},{1,5},{2,0},{3,7},{4,6},{5,1},{6,4},{7,3}} | collective-permute-start | bytes 6291464 | tf_op jit(solution)/shard_map/ppermute | solution.py:233
  337.6 65.1 %collective-permute-start.16 = (f32[8256,128]{1,0:T(8,128)}, f32[8256,128]{1,0:T(8,128)}, u32[]{:S(2)}, u32[]{:S(2)}) collective-permute-start(f32[8256,128]{1,0:T(8,128)} %get-tuple-element.57), channel_id=1, source_target_pairs={{0,1},{1,0},{2,3},{3,2},{4,5},{5,4},{6,7},{7,6}} | collective-permute-start | bytes 12681224 | tf_op jit(solution)/shard_map/ppermute | solution.py:233
  402.7 90.6 %collective-permute-start.12 = (f32[8256,128]{1,0:T(8,128)}, f32[8256,128]{1,0:T(8,128)}, u32[]{:S(2)}, u32[]{:S(2)}) collective-permute-start(f32[8256,128]{1,0:T(8,128)} %get-tuple-element.52), channel_id=1, source_target_pairs={{0,1},{1,0},{2,3},{3,2},{4,5},{5,4},{6,7},{7,6}} | collective-permute-start | bytes 12681224 | tf_op jit(solution)/shard_map/ppermute | solution.py:233
  408.2 40.1 %collective-permute-start.19 = (f32[4096,128]{1,0:T(8,128)S(1)}, f32[4096,128]{1,0:T(8,128)S(1)}, u32[]{:S(2)}, u32[]{:S(2)}) collective-permute-start(f32[4096,128]{1,0:T(8,128)S(1)} %slice_add_fusion), channel_id=1, source_target_pairs={{0,4},{1,3},{2,6},{3,1},{4,0},{5,7},{6,2},{7,5}} | collective-permute-start | bytes 6291464 | tf_op jit(solution)/shard_map/ppermute | solution.py:233
  408.3 100.6 %collective-permute-start.5 = (f32[8256,128]{1,0:T(8,128)}, f32[8256,128]{1,0:T(8,128)}, u32[]{:S(2)}, u32[]{:S(2)}) collective-permute-start(f32[8256,128]{1,0:T(8,128)} %get-tuple-element.44), channel_id=1, source_target_pairs={{0,1},{1,0},{2,3},{3,2},{4,5},{5,4},{6,7},{7,6}} | collective-permute-start | bytes 12681224 | tf_op jit(solution)/shard_map/ppermute | solution.py:233
  409.1 86.2 %slice-start.4 = ((s8[4227072]{0:T(1024)(128)(4,1)}), s8[4194304]{0:T(1024)(128)(4,1)S(1)}, s32[]{:S(2)}) async-start(s8[4227072]{0:T(1024)(128)(4,1)} %bitcast.23), calls=%async_computation.5 | async-start | bytes 8388608
  412.4 5.7 %copy-start = (f32[4096,128]{1,0:T(8,128)S(1)}, f32[4096,128]{1,0:T(8,128)}, u32[]{:S(2)}) copy-start(f32[4096,128]{1,0:T(8,128)} %slice_add_fusion.8.refs_10_) | copy-start | bytes 6291460
  412.4 82.9 %slice-start.5 = ((s8[4227072]{0:T(1024)(128)(4,1)}), s8[32768]{0:T(1024)(128)(4,1)S(1)}, s32[]{:S(2)}) async-start(s8[4227072]{0:T(1024)(128)(4,1)} %bitcast.23), calls=%async_computation.6 | async-start | bytes 65536
  412.4 80.9 %collective-permute-start.18 = (f32[4096,128]{1,0:T(8,128)S(1)}, f32[4096,128]{1,0:T(8,128)S(1)}, u32[]{:S(2)}, u32[]{:S(2)}) collective-permute-start(f32[4096,128]{1,0:T(8,128)S(1)} %add_add_fusion), channel_id=1, source_target_pairs={{0,4},{1,3},{2,6},{3,1},{4,0},{5,7},{6,2},{7,5}} | collective-permute-start | bytes 6291464 | tf_op jit(solution)/shard_map/ppermute | solution.py:233
  418.1 75.2 %copy-start.1 = (f32[4096,128]{1,0:T(8,128)S(1)}, f32[4096,128]{1,0:T(8,128)}, u32[]{:S(2)}) copy-start(f32[4096,128]{1,0:T(8,128)} %slice_add_fusion.7.refs_9_) | copy-start | bytes 6291460
  418.1 85.6 %collective-permute-start.6 = (f32[4096,128]{1,0:T(8,128)S(1)}, f32[4096,128]{1,0:T(8,128)}, u32[]{:S(2)}, u32[]{:S(2)}) collective-permute-start(f32[4096,128]{1,0:T(8,128)S(1)} %copy-done), channel_id=1, source_target_pairs={{0,2},{1,5},{2,0},{3,7},{4,6},{5,1},{6,4},{7,3}} | collective-permute-start | bytes 6291464 | tf_op jit(solution)/shard_map/ppermute | solution.py:233
  448.4 60.5 %collective-permute-start.8 = (f32[4096,128]{1,0:T(8,128)}, f32[4096,128]{1,0:T(8,128)}, u32[]{:S(2)}, u32[]{:S(2)}) collective-permute-start(f32[4096,128]{1,0:T(8,128)} %add_add_fusion.3), channel_id=1, source_target_pairs={{0,2},{1,5},{2,0},{3,7},{4,6},{5,1},{6,4},{7,3}} | collective-permute-start | bytes 6291464 | tf_op jit(solution)/shard_map/ppermute | solution.py:233
  493.3 30.9 %collective-permute-start.11 = (f32[4096,128]{1,0:T(8,128)S(1)}, f32[4096,128]{1,0:T(8,128)S(1)}, u32[]{:S(2)}, u32[]{:S(2)}) collective-permute-start(f32[4096,128]{1,0:T(8,128)S(1)} %copy-done.1), channel_id=1, source_target_pairs={{0,4},{1,3},{2,6},{3,1},{4,0},{5,7},{6,2},{7,5}} | collective-permute-start | bytes 6291464 | tf_op jit(solution)/shard_map/ppermute | solution.py:233
  493.3 53.3 %collective-permute-start.10 = (f32[4096,128]{1,0:T(8,128)}, f32[4096,128]{1,0:T(8,128)S(1)}, u32[]{:S(2)}, u32[]{:S(2)}) collective-permute-start(f32[4096,128]{1,0:T(8,128)} %add_add_fusion.2), channel_id=1, source_target_pairs={{0,4},{1,3},{2,6},{3,1},{4,0},{5,7},{6,2},{7,5}} | collective-permute-start | bytes 6291464 | tf_op jit(solution)/shard_map/ppermute | solution.py:233
  499.8 9.1 %slice-start.2 = ((s8[4227072]{0:T(1024)(128)(4,1)}), s8[4194304]{0:T(1024)(128)(4,1)S(1)}, s32[]{:S(2)}) async-start(s8[4227072]{0:T(1024)(128)(4,1)} %bitcast.21), calls=%async_computation.3 | async-start | bytes 8388608
  499.8 9.1 %slice-start.3 = ((s8[4227072]{0:T(1024)(128)(4,1)}), s8[32768]{0:T(1024)(128)(4,1)S(1)}, s32[]{:S(2)}) async-start(s8[4227072]{0:T(1024)(128)(4,1)} %bitcast.21), calls=%async_computation.4 | async-start | bytes 65536

commit v3 on v2

--- a/solution.py
+++ b/solution.py
@@ -1,3 +1,5 @@
+import functools
+
 import jax
 import jax.numpy as jnp
 from jax import lax
@@ -66,10 +68,11 @@
         for k in range(3):
             fetch(k, 0, 0).start()
 
-    @pl.when(e + 1 < n_exp)
-    def _():
-        for k in range(3):
-            fetch(k, e + 1, 1 - slot).start()
+    def fetch_next(ks):
+        @pl.when(e + 1 < n_exp)
+        def _():
+            for k in ks:
+                fetch(k, e + 1, 1 - slot).start()
 
     @pl.when(e == 0)
     def _():
@@ -95,6 +98,7 @@
 
     fetch(0, e, slot).wait()
     fetch(1, e, slot).wait()
+    fetch_next((0, 1))
     wg_ref, wu_ref, wd_ref = (buf.at[slot] for buf in bufs)
 
     def hidden(r0, rows):
@@ -105,6 +109,7 @@
 
     row_chunks(total, hidden)
     fetch(2, e, slot).wait()
+    fetch_next((2,))
 
     def result(r0, rows):
         for jj in range(wd_ref.shape[1] // 256):
@@ -177,46 +182,72 @@
     )(src, core, count, x, x, addr, addr, wt, wt, wg, wu, wd, *after)
 
 
-def final_kernel(a1_ref, a2_ref, b1_ref, b2_ref, *rest):
+def chip_sum_kernel(low_half, own_ref, sib_ref, relay_ref, out_ref):
+    in_low = pl.program_id(0) < pl.num_programs(0) // 2
+    relayed = in_low if low_half else jnp.logical_not(in_low)
+
+    @pl.when(relayed)
+    def _():
+        out_ref[...] = own_ref[...] + sib_ref[...] + relay_ref[...]
+
+    @pl.when(jnp.logical_not(relayed))
+    def _():
+        out_ref[...] = own_ref[...] + sib_ref[...]
+
+
+def chip_sum(own, sib, relay, low_half):
+    rows = 2 * relay.shape[0]
+    steps = 2
+    block = rows // steps
+    half = steps // 2
+    if low_half:
+        relay_map = lambda t: (jnp.minimum(t, half - 1), 0)
+    else:
+        relay_map = lambda t: (jnp.maximum(t - half, 0), 0)
+    spec = pl.BlockSpec((block, LANES), lambda t: (t, 0))
+    return pl.pallas_call(
+        functools.partial(chip_sum_kernel, low_half),
+        grid=(steps,),
+        in_specs=[spec, spec, pl.BlockSpec((block, LANES), relay_map)],
+        out_specs=spec,
+        out_shape=jax.ShapeDtypeStruct((rows, LANES), jnp.float32),
+        compiler_params=pltpu.CompilerParams(dimension_semantics=('arbitrary',), vmem_limit_bytes=60 * 2 ** 20),
+        cost_estimate=pl.CostEstimate(flops=10 ** 7, transcendentals=0, bytes_accessed=rows * LANES * 14),
+        name='chip_sum',
+    )(own, sib, relay)
+
+
+def final_kernel(a_ref, b_ref, *rest):
     out_ref, s_ref = rest[-2:]
-    step = pl.program_id(0)
-    half = pl.num_programs(0) // 2
-
-    def emit(a_ref, b_ref):
-        def body(b, carry):
-            r = pl.ds(pl.multiple_of(b * 16 * JT, 16 * JT), 16 * JT)
-            s_ref[r, :] = a_ref[r, :] + b_ref[r, :]
-            for j in range(JT):
-                pair = [s_ref[pl.ds((b * 16 + k) * JT + j, 8, stride=JT), :] for k in (0, 8)]
-                out_ref[pl.ds(pl.multiple_of(b * 16, 16), 16), j * LANES:(j + 1) * LANES] = (
-                    jnp.concatenate(pair, axis=0).astype(out_ref.dtype))
-            return carry
-
-        lax.fori_loop(0, out_ref.shape[0] // 16, body, 0)
-
-    pl.when(step < half)(lambda: emit(a1_ref, b1_ref))
-    pl.when(step >= half)(lambda: emit(a2_ref, b2_ref))
-
-
-def final_sum(a1, a2, b1, b2, n, n_tok, width, out):
-    tb = 128
-    steps = n_tok // tb
-    half = steps // 2
-    low = pl.BlockSpec((tb * JT, LANES), lambda i: (jnp.minimum(i, half - 1), 0))
-    high = pl.BlockSpec((tb * JT, LANES), lambda i: (jnp.maximum(i - half, 0), 0))
+
+    def body(b, carry):
+        r = pl.ds(pl.multiple_of(b * 16 * JT, 16 * JT), 16 * JT)
+        s_ref[r, :] = a_ref[r, :] + b_ref[r, :]
+        for j in range(JT):
+            pair = [s_ref[pl.ds((b * 16 + k) * JT + j, 8, stride=JT), :] for k in (0, 8)]
+            out_ref[pl.ds(pl.multiple_of(b * 16, 16), 16), j * LANES:(j + 1) * LANES] = (
+                jnp.concatenate(pair, axis=0).astype(out_ref.dtype))
+        return carry
+
+    lax.fori_loop(0, out_ref.shape[0] // 16, body, 0, unroll=4)
+
+
+def final_sum(a, b, n, n_tok, width, out):
+    tb = 256
+    spec = pl.BlockSpec((tb * JT, LANES), lambda i: (i, 0))
     prior = [] if out is None else [out]
     return pl.pallas_call(
         final_kernel,
-        grid=(steps,),
-        in_specs=[low, high, low, high] + [pl.BlockSpec(memory_space=ANY)] * len(prior),
+        grid=(n_tok // tb,),
+        in_specs=[spec, spec] + [pl.BlockSpec(memory_space=ANY)] * len(prior),
         out_specs=pl.BlockSpec((tb, COLS), lambda i: (i, n)),
         scratch_shapes=[pltpu.VMEM((tb * JT, LANES), jnp.float32)],
         out_shape=jax.ShapeDtypeStruct((n_tok, width), jnp.bfloat16),
-        input_output_aliases={4: 0} if prior else {},
+        input_output_aliases={2: 0} if prior else {},
         compiler_params=pltpu.CompilerParams(dimension_semantics=('arbitrary',), vmem_limit_bytes=30 * 2 ** 20),
         cost_estimate=pl.CostEstimate(flops=10 ** 7, transcendentals=0, bytes_accessed=n_tok * COLS * 10),
         name='final_sum',
-    )(a1, a2, b1, b2, *prior)
+    )(a, b, *prior)
 
 
 def solution(mesh):
@@ -264,22 +295,19 @@
 
         got, got2, after2 = [], [], []
         for n, (own, sib) in zip(blocks, ffn((1, 2), gate)):
-            low = own[lo] + sib[lo]
-            own, sib, relayed = lax.optimization_barrier((own, sib, relay_hi[n]))
-            got.append((send(low, straight),
-                        send(own[hi] + sib[hi] + relayed, straight)))
-            after2.append(low)
+            total = chip_sum(own, sib, relay_hi[n], False)
+            got.append(send(total, straight))
+            after2.append(total)
+        gate = []
         for n, (own, sib) in zip(blocks, ffn((2, 1), after2)):
-            high = own[hi] + sib[hi]
-            own, sib, relayed = lax.optimization_barrier((own, sib, relay_lo[n]))
-            got2.append((send(own[lo] + sib[lo] + relayed, crossed),
-                         send(high, crossed)))
-            gate = [high]
+            total = chip_sum(own, sib, relay_lo[n], True)
+            got2.append(send(total, crossed))
+            gate.append(total)
 
         out = None
         for n, (own, sib) in zip(blocks, ffn((0, 0), gate)):
-            out = final_sum(own[lo] + sib[lo] + got[n][0], own[hi] + sib[hi] + got[n][1],
-                            got2[n][0], got2[n][1], n, n_tok, width, out)
+            early = own[:n_tok * JT] + sib[:n_tok * JT] + got[n]
+            out = final_sum(early, got2[n], n, n_tok, width, out)
         return out
 
     return jax.shard_map(local_part, mesh=mesh,

time: 551 us -> 590 us (1.071)
  waiting for transfers between devices: 213 us -> 264 us
  other arithmetic: 56.6 us -> 24.7 us
  Pallas kernels: 253 us -> 273 us
    ppermute x20 -> x16, waiting for transfers between devices: 208 us -> 259 us  [send(): return lax.ppermute(a, GROUP_AXES, pairs)]
    add x10 -> x2, other arithmetic: 38.8 us -> 6.98 us  [local_part(): early = own[:n_tok * JT] + sib[:n_tok * JT] + got[n]]
    pallas_call x2 -> x6, Pallas kernels: 7.69 us -> 28.1 us  [the longest x4 22.8 us: chip_sum(): pl.pallas_call(functools.partial(chip_sum_kernel, low_half), grid=(steps,...]
    ppermute x20 -> x16, starting transfers between devices: 19.4 us -> 15.2 us  [send(): return lax.ppermute(a, GROUP_AXES, pairs)]
  transfers between devices with their start and end apart: 21 -> 17, of which waited for: 12 -> 8; matrix products, arithmetic and copies ran while one was open for 8% -> 3% of each run, Pallas kernels for 12% -> 2%
where the time goes in v3:
time: 590 us
  Pallas kernels  273 us (46%)
  waiting for transfers between devices  264 us (45%)
  other arithmetic  24.7 us (4%)
  starting transfers between devices  19.5 us (3%)
    ppermute x16, waiting for transfers between devices, send(): return lax.ppermute(a, GROUP_AXES, pairs)  259 us
    pallas_call x4, Pallas kernels, ffn_pass(): pl.pallas_call(pass_kernel, grid_spec=pltpu.PrefetchScalarGridSpec(num_sc...  245 us
    pallas_call x4, Pallas kernels, chip_sum(): pl.pallas_call(functools.partial(chip_sum_kernel, low_half), grid=(steps,...  22.8 us
    ppermute x16, starting transfers between devices, send(): return lax.ppermute(a, GROUP_AXES, pairs)  15.2 us
  transfers between devices with their start and end apart: 17, of which 8 were waited for; matrix products, arithmetic and copies ran while one was open for 3% of the time, Pallas kernels for 2%

profile of v3, /device:TPU:0, one launch (start us, length us, event | category | flops | bytes accessed | tf_op | source)
XLA Modules:
  0.0 589.8 jit_solution(5902248139818739405)
XLA Ops:
  0.0 2.7 fusion.7
  2.7 3.2 fusion.9
  5.9 0.1 fusion.14
  6.0 0.1 copy.14
  6.2 0.1 copy.12
  6.3 0.8 maximum_bitcast_fusion
  7.1 4.3 all-to-all-start
  11.4 0.6 pad_add_fusion.3.src_ref
  12.1 4.8 all-to-all-done
  16.9 0.1 slice_compare_fusion
  17.0 0.2 select_reduce_fusion
  17.2 0.6 reshape.33.n_ref
  17.8 0.7 slice_bitcast_fusion
  18.6 61.0 %ffn_pass.4 = (f32[8256,128]{1,0:T(8,128)}, f32[8256,128]{1,0:T(8,128)}, f32[8256,128]{1,0:T(8,128)}, f32[8256,128]{1,0:T(8,128)}) custom-call(s32[2]{0:T(128)} %pad_add_fusion.3.src_ref, s32[1]{0:T(128)} %bitcast.2.core_ref, s32[64]{0:T(128)} %reshape.33.n_ref, bf16[8,8,192,2048]{3,2,1,0:T(8,128)(2,1)} %refs_1_.7, bf16[8,8,192,2048]{3,2,1,0:T(8,128)(2,1)} %refs_1_.7, ...), custom_call_target="tpu_custom_call" | custom-call | flops 53150220288 | bytes 138412032 | tf_op jit(solution)/shard_map/ffn_pass/pallas_call | solution.py:164
  79.6 2.0 collective-permute-start.1
  81.6 0.6 pad_add_fusion.2.src_ref
  82.2 6.6 %collective-permute-done.1 = f32[8256,128]{1,0:T(8,128)} collective-permute-done((f32[8256,128]{1,0:T(8,128)}, f32[8256,128]{1,0:T(8,128)}, u32[]{:S(2)}, u32[]{:S(2)}) %collective-permute-start.1) | collective-permute-done | bytes 4227104 | tf_op jit(solution)/shard_map/ppermute | solution.py:264
  88.7 6.0 %slice_add_fusion.2 = (f32[4096,128]{1,0:T(8,128)}, f32[4096,128]{1,0:T(8,128)}) fusion(f32[8256,128]{1,0:T(8,128)} %collective-permute-done.1, f32[8256,128]{1,0:T(8,128)} %get-tuple-element.23), kind=kLoop, calls=%fused_computation.13 | loop fusion | flops 1048576 | bytes 12582912 | tf_op jit(solution)/shard_map/add | solution.py:291
  94.8 4.8 slice_add_fusion.3
  99.6 61.2 %ffn_pass.5 = (f32[8256,128]{1,0:T(8,128)}, f32[8256,128]{1,0:T(8,128)}, f32[8256,128]{1,0:T(8,128)}, f32[8256,128]{1,0:T(8,128)}) custom-call(s32[2]{0:T(128)} %pad_add_fusion.2.src_ref, s32[1]{0:T(128)} %bitcast.2.core_ref, s32[64]{0:T(128)} %reshape.33.n_ref, bf16[8,8,192,2048]{3,2,1,0:T(8,128)(2,1)} %refs_1_.7, bf16[8,8,192,2048]{3,2,1,0:T(8,128)(2,1)} %refs_1_.7, ...), custom_call_target="tpu_custom_call" | custom-call | flops 53150220288 | bytes 138412032 | tf_op jit(solution)/shard_map/ffn_pass/pallas_call | solution.py:164
  160.7 2.8 collective-permute-start.2
  163.6 2.0 collective-permute-start.5
  165.6 0.6 pad_add_fusion.1.src_ref
  166.3 23.7 %collective-permute-done.3.relay_ref = f32[4096,128]{1,0:T(8,128)} collective-permute-done((f32[4096,128]{1,0:T(8,128)}, f32[4096,128]{1,0:T(8,128)}, u32[]{:S(2)}, u32[]{:S(2)}) %collective-permute-start.3) | collective-permute-done | bytes 2097184 | tf_op jit(solution)/shard_map/ppermute | solution.py:264
  190.0 5.7 chip_sum.4.refs_9_
  195.7 16.7 %collective-permute-done.5.relay_ref = f32[4096,128]{1,0:T(8,128)S(1)} collective-permute-done((f32[4096,128]{1,0:T(8,128)}, f32[4096,128]{1,0:T(8,128)S(1)}, u32[]{:S(2)}, u32[]{:S(2)}) %collective-permute-start.5) | collective-permute-done | bytes 2097184 | tf_op jit(solution)/shard_map/ppermute | solution.py:264
  212.3 1.3 copy-done.4
  213.7 5.8 chip_sum.5.refs_10_
  219.4 61.3 %ffn_pass.6 = (f32[8256,128]{1,0:T(8,128)}, f32[8256,128]{1,0:T(8,128)}, f32[8256,128]{1,0:T(8,128)}, f32[8256,128]{1,0:T(8,128)}) custom-call(s32[2]{0:T(128)} %pad_add_fusion.1.src_ref, s32[1]{0:T(128)} %bitcast.2.core_ref, s32[64]{0:T(128)} %reshape.33.n_ref, bf16[8,8,192,2048]{3,2,1,0:T(8,128)(2,1)} %refs_1_.7, bf16[8,8,192,2048]{3,2,1,0:T(8,128)(2,1)} %refs_1_.7, ...), custom_call_target="tpu_custom_call" | custom-call | flops 53150220288 | bytes 138412032 | tf_op jit(solution)/shard_map/ffn_pass/pallas_call | solution.py:164
  280.8 2.1 collective-permute-start.8
  282.9 2.0 collective-permute-start.7
  284.9 0.6 pad_add_fusion.src_ref
  285.5 23.7 %collective-permute-done.9.relay_ref = f32[4096,128]{1,0:T(8,128)} collective-permute-done((f32[4096,128]{1,0:T(8,128)}, f32[4096,128]{1,0:T(8,128)}, u32[]{:S(2)}, u32[]{:S(2)}) %collective-permute-start.9) | collective-permute-done | bytes 2097184 | tf_op jit(solution)/shard_map/ppermute | solution.py:264
  309.2 5.6 chip_sum.7.refs_10_
  314.9 16.7 %collective-permute-done.7.relay_ref = f32[4096,128]{1,0:T(8,128)S(1)} collective-permute-done((f32[4096,128]{1,0:T(8,128)}, f32[4096,128]{1,0:T(8,128)S(1)}, u32[]{:S(2)}, u32[]{:S(2)}) %collective-permute-start.7) | collective-permute-done | bytes 2097184 | tf_op jit(solution)/shard_map/ppermute | solution.py:264
  331.6 1.3 copy-done.3
  332.9 5.7 chip_sum.6.refs_9_
  338.6 61.2 %ffn_pass.7 = (f32[8256,128]{1,0:T(8,128)}, f32[8256,128]{1,0:T(8,128)}, f32[8256,128]{1,0:T(8,128)}, f32[8256,128]{1,0:T(8,128)}) custom-call(s32[2]{0:T(128)} %pad_add_fusion.src_ref, s32[1]{0:T(128)} %bitcast.2.core_ref, s32[64]{0:T(128)} %reshape.33.n_ref, bf16[8,8,192,2048]{3,2,1,0:T(8,128)(2,1)} %refs_1_.7, bf16[8,8,192,2048]{3,2,1,0:T(8,128)(2,1)} %refs_1_.7, ...), custom_call_target="tpu_custom_call" | custom-call | flops 53150220288 | bytes 138412032 | tf_op jit(solution)/shard_map/ffn_pass/pallas_call | solution.py:164
  399.8 2.1 collective-permute-start.13
  402.0 1.7 collective-permute-start.15
  403.7 0.3 collective-permute-start.11
  404.0 91.4 %collective-permute-done.14 = f32[8192,128]{1,0:T(8,128)S(1)} collective-permute-done((f32[8192,128]{1,0:T(8,128)}, f32[8192,128]{1,0:T(8,128)S(1)}, u32[]{:S(2)}, u32[]{:S(2)}) %collective-permute-start.14) | collective-permute-done | bytes 4194336 | tf_op jit(solution)/shard_map/ppermute | solution.py:264
  495.4 1.9 copy-done.2
  497.4 4.1 fusion.1.a_ref
  501.5 2.7 final_sum.2.rest_0_
  504.1 80.0 %collective-permute-done.11 = f32[8192,128]{1,0:T(8,128)S(1)} collective-permute-done((f32[8192,128]{1,0:T(8,128)}, f32[8192,128]{1,0:T(8,128)S(1)}, u32[]{:S(2)}, u32[]{:S(2)}) %collective-permute-start.11) | collective-permute-done | bytes 4194336 | tf_op jit(solution)/shard_map/ppermute | solution.py:264
  584.2 2.9 fusion.2.a_ref
  587.1 2.7 final_sum.3
  (31 shorter events, 0.4 us)
Async XLA Ops:
  0.0 2.7 copy-start.5
  7.1 9.8 %all-to-all-start = ((f32[8,2,8,192]{3,1,2,0:T(2,128)}), f32[8,2,8,192]{3,1,2,0:T(2,128)S(1)}, u32[]{:S(2)}, u32[]{:S(2)}) async-start(f32[8,2,8,192]{3,1,2,0:T(2,128)} %maximum_bitcast_fusion), calls=%async_computation | async-start | bytes 262144 | tf_op jit(solution)/shard_map/all_to_all | solution.py:274
  79.6 9.2 %collective-permute-start.1 = (f32[8256,128]{1,0:T(8,128)}, f32[8256,128]{1,0:T(8,128)}, u32[]{:S(2)}, u32[]{:S(2)}) collective-permute-start(f32[8256,128]{1,0:T(8,128)} %get-tuple-element.24), channel_id=1, source_target_pairs={{0,1},{1,0},{2,3},{3,2},{4,5},{5,4},{6,7},{7,6}} | collective-permute-start | bytes 12681224 | tf_op jit(solution)/shard_map/ppermute | solution.py:264
  81.6 13.2 %collective-permute-start = (f32[8256,128]{1,0:T(8,128)}, f32[8256,128]{1,0:T(8,128)}, u32[]{:S(2)}, u32[]{:S(2)}) collective-permute-start(f32[8256,128]{1,0:T(8,128)} %get-tuple-element.22), channel_id=1, source_target_pairs={{0,1},{1,0},{2,3},{3,2},{4,5},{5,4},{6,7},{7,6}} | collective-permute-start | bytes 12681224 | tf_op jit(solution)/shard_map/ppermute | solution.py:264
  88.7 6.0 %copy-start = (f32[8256,128]{1,0:T(8,128)S(1)}, f32[8256,128]{1,0:T(8,128)}, u32[]{:S(2)}) copy-start(f32[8256,128]{1,0:T(8,128)} %get-tuple-element.21) | copy-start | bytes 12681220
  160.7 29.2 %collective-permute-start.2 = (f32[8256,128]{1,0:T(8,128)}, f32[8256,128]{1,0:T(8,128)}, u32[]{:S(2)}, u32[]{:S(2)}) collective-permute-start(f32[8256,128]{1,0:T(8,128)} %get-tuple-element.26), channel_id=1, source_target_pairs={{0,1},{1,0},{2,3},{3,2},{4,5},{5,4},{6,7},{7,6}} | collective-permute-start | bytes 12681224 | tf_op jit(solution)/shard_map/ppermute | solution.py:264
  163.6 48.8 %collective-permute-start.4 = (f32[8256,128]{1,0:T(8,128)}, f32[8256,128]{1,0:T(8,128)}, u32[]{:S(2)}, u32[]{:S(2)}) collective-permute-start(f32[8256,128]{1,0:T(8,128)} %get-tuple-element.28), channel_id=1, source_target_pairs={{0,1},{1,0},{2,3},{3,2},{4,5},{5,4},{6,7},{7,6}} | collective-permute-start | bytes 12681224 | tf_op jit(solution)/shard_map/ppermute | solution.py:264
  163.6 26.4 %collective-permute-start.3 = (f32[4096,128]{1,0:T(8,128)}, f32[4096,128]{1,0:T(8,128)}, u32[]{:S(2)}, u32[]{:S(2)}) collective-permute-start(f32[4096,128]{1,0:T(8,128)} %get-tuple-element.37), channel_id=1, source_target_pairs={{0,4},{1,3},{2,6},{3,1},{4,0},{5,7},{6,2},{7,5}} | collective-permute-start | bytes 6291464 | tf_op jit(solution)/shard_map/ppermute | solution.py:264
  163.6 48.7 %collective-permute-start.5 = (f32[4096,128]{1,0:T(8,128)}, f32[4096,128]{1,0:T(8,128)S(1)}, u32[]{:S(2)}, u32[]{:S(2)}) collective-permute-start(f32[4096,128]{1,0:T(8,128)} %get-tuple-element.39), channel_id=1, source_target_pairs={{0,4},{1,3},{2,6},{3,1},{4,0},{5,7},{6,2},{7,5}} | collective-permute-start | bytes 6291464 | tf_op jit(solution)/shard_map/ppermute | solution.py:264
  212.3 1.3 copy-start.4
  280.8 28.5 %collective-permute-start.8 = (f32[8256,128]{1,0:T(8,128)}, f32[8256,128]{1,0:T(8,128)}, u32[]{:S(2)}, u32[]{:S(2)}) collective-permute-start(f32[8256,128]{1,0:T(8,128)} %get-tuple-element.32), channel_id=1, source_target_pairs={{0,1},{1,0},{2,3},{3,2},{4,5},{5,4},{6,7},{7,6}} | collective-permute-start | bytes 12681224 | tf_op jit(solution)/shard_map/ppermute | solution.py:264
  282.9 48.8 %collective-permute-start.6 = (f32[8256,128]{1,0:T(8,128)}, f32[8256,128]{1,0:T(8,128)}, u32[]{:S(2)}, u32[]{:S(2)}) collective-permute-start(f32[8256,128]{1,0:T(8,128)} %get-tuple-element.30), channel_id=1, source_target_pairs={{0,1},{1,0},{2,3},{3,2},{4,5},{5,4},{6,7},{7,6}} | collective-permute-start | bytes 12681224 | tf_op jit(solution)/shard_map/ppermute | solution.py:264
  282.9 26.4 %collective-permute-start.9 = (f32[4096,128]{1,0:T(8,128)}, f32[4096,128]{1,0:T(8,128)}, u32[]{:S(2)}, u32[]{:S(2)}) collective-permute-start(f32[4096,128]{1,0:T(8,128)} %get-tuple-element.40.refs_10_), channel_id=1, source_target_pairs={{0,2},{1,5},{2,0},{3,7},{4,6},{5,1},{6,4},{7,3}} | collective-permute-start | bytes 6291464 | tf_op jit(solution)/shard_map/ppermute | solution.py:264
  282.9 48.7 %collective-permute-start.7 = (f32[4096,128]{1,0:T(8,128)}, f32[4096,128]{1,0:T(8,128)S(1)}, u32[]{:S(2)}, u32[]{:S(2)}) collective-permute-start(f32[4096,128]{1,0:T(8,128)} %get-tuple-element.38.refs_9_), channel_id=1, source_target_pairs={{0,2},{1,5},{2,0},{3,7},{4,6},{5,1},{6,4},{7,3}} | collective-permute-start | bytes 6291464 | tf_op jit(solution)/shard_map/ppermute | solution.py:264
  331.6 1.3 copy-start.3
  399.8 95.6 %collective-permute-start.13 = (f32[8256,128]{1,0:T(8,128)}, f32[8256,128]{1,0:T(8,128)S(1)}, u32[]{:S(2)}, u32[]{:S(2)}) collective-permute-start(f32[8256,128]{1,0:T(8,128)} %get-tuple-element.36), channel_id=1, source_target_pairs={{0,1},{1,0},{2,3},{3,2},{4,5},{5,4},{6,7},{7,6}} | collective-permute-start | bytes 12681224 | tf_op jit(solution)/shard_map/ppermute | solution.py:264
  402.0 93.5 %collective-permute-start.14 = (f32[8192,128]{1,0:T(8,128)}, f32[8192,128]{1,0:T(8,128)S(1)}, u32[]{:S(2)}, u32[]{:S(2)}) collective-permute-start(f32[8192,128]{1,0:T(8,128)} %chip_sum.4.refs_9_), channel_id=1, source_target_pairs={{0,2},{1,5},{2,0},{3,7},{4,6},{5,1},{6,4},{7,3}} | collective-permute-start | bytes 12582920 | tf_op jit(solution)/shard_map/ppermute | solution.py:264
  402.0 182.2 %collective-permute-start.10 = (f32[8256,128]{1,0:T(8,128)}, f32[8256,128]{1,0:T(8,128)}, u32[]{:S(2)}, u32[]{:S(2)}) collective-permute-start(f32[8256,128]{1,0:T(8,128)} %get-tuple-element.34), channel_id=1, source_target_pairs={{0,1},{1,0},{2,3},{3,2},{4,5},{5,4},{6,7},{7,6}} | collective-permute-start | bytes 12681224 | tf_op jit(solution)/shard_map/ppermute | solution.py:264
  402.0 99.4 %collective-permute-start.15 = (f32[8192,128]{1,0:T(8,128)}, f32[8192,128]{1,0:T(8,128)S(1)}, u32[]{:S(2)}, u32[]{:S(2)}) collective-permute-start(f32[8192,128]{1,0:T(8,128)} %chip_sum.6.refs_9_), channel_id=1, source_target_pairs={{0,4},{1,3},{2,6},{3,1},{4,0},{5,7},{6,2},{7,5}} | collective-permute-start | bytes 12582920 | tf_op jit(solution)/shard_map/ppermute | solution.py:264
  403.7 180.4 %collective-permute-start.11 = (f32[8192,128]{1,0:T(8,128)}, f32[8192,128]{1,0:T(8,128)S(1)}, u32[]{:S(2)}, u32[]{:S(2)}) collective-permute-start(f32[8192,128]{1,0:T(8,128)} %chip_sum.5.refs_10_), channel_id=1, source_target_pairs={{0,2},{1,5},{2,0},{3,7},{4,6},{5,1},{6,4},{7,3}} | collective-permute-start | bytes 12582920 | tf_op jit(solution)/shard_map/ppermute | solution.py:264
  495.4 91.7 %collective-permute-start.12 = (f32[8192,128]{1,0:T(8,128)}, f32[8192,128]{1,0:T(8,128)S(1)}, u32[]{:S(2)}, u32[]{:S(2)}) collective-permute-start(f32[8192,128]{1,0:T(8,128)} %chip_sum.7.refs_10_), channel_id=1, source_target_pairs={{0,4},{1,3},{2,6},{3,1},{4,0},{5,7},{6,2},{7,5}} | collective-permute-start | bytes 12582920 | tf_op jit(solution)/shard_map/ppermute | solution.py:264
  495.4 1.9 copy-start.2
  501.4 82.7 %copy-start.1 = (f32[8256,128]{1,0:T(8,128)S(1)}, f32[8256,128]{1,0:T(8,128)}, u32[]{:S(2)}) copy-start(f32[8256,128]{1,0:T(8,128)} %get-tuple-element.33) | copy-start | bytes 12681220

commit v4 on v3

--- a/solution.py
+++ b/solution.py
@@ -53,19 +53,21 @@
 
 
 def pass_kernel(src_ref, core_ref, n_ref, *refs):
-    x_refs, addr_refs, wt_refs, weights = refs[0:2], refs[2:4], refs[4:6], refs[6:9]
-    outs, bufs, (h_ref, xs_ref, y_ref, acc_ref, w_sem, sem) = refs[-13:-9], refs[-9:-6], refs[-6:]
+    x_ref, addr_refs, wt_refs, weights = refs[0], refs[1:3], refs[3:5], refs[5:8]
+    outs, bufs, (x_buf, h_ref, xs_ref, y_ref, acc_ref, w_sem, sem) = refs[-14:-10], refs[-10:-7], refs[-7:]
     ff = h_ref.shape[1]
     e = pl.program_id(0)
     n_exp = pl.num_programs(0)
     slot = e % 2
 
     def fetch(k, expert, into):
+        if k >= 3:
+            return pltpu.make_async_copy(x_ref.at[src_ref[k - 3], expert], x_buf.at[into, k - 3], w_sem.at[into, k])
         return pltpu.make_async_copy(weights[k].at[expert], bufs[k].at[into], w_sem.at[into, k])
 
     @pl.when(e == 0)
     def _():
-        for k in range(3):
+        for k in (3, 4, 0, 1, 2):
             fetch(k, 0, 0).start()
 
     def fetch_next(ks):
@@ -89,16 +91,18 @@
     total = first[1] + round16(counts[1])
 
     for i in range(2):
+        fetch(3 + i, e, slot).wait()
+
         def copy(b, carry):
             xs_ref[pl.ds(pl.multiple_of(first[i] + b * 16, 16), 16), :] = (
-                x_refs[i][0, 0, pl.ds(pl.multiple_of(b * 16, 16), 16), :])
+                x_buf[slot, i, pl.ds(pl.multiple_of(b * 16, 16), 16), :])
             return carry
 
         lax.fori_loop(0, round16(counts[i]) // 16, copy, 0)
 
     fetch(0, e, slot).wait()
     fetch(1, e, slot).wait()
-    fetch_next((0, 1))
+    fetch_next((3, 4, 0, 1))
     wg_ref, wu_ref, wd_ref = (buf.at[slot] for buf in bufs)
 
     def hidden(r0, rows):
@@ -158,28 +162,28 @@
     rows = 2 * slots
     acc_rows = (n_tok + 8) * JT
     acc = jax.ShapeDtypeStruct((acc_rows, LANES), jnp.float32)
-    x_specs = [pl.BlockSpec((1, 1, slots, width), lambda e, src, *_, i=i: (src[i], e, 0, 0)) for i in range(2)]
     table_specs = [pl.BlockSpec((1, 1, 1, slots), lambda e, src, *_, i=i: (src[i], e, 0, 0),
                                 memory_space=pltpu.SMEM) for i in range(2)]
     return pl.pallas_call(
         pass_kernel,
         grid_spec=pltpu.PrefetchScalarGridSpec(
             num_scalar_prefetch=3, grid=(n_exp,),
-            in_specs=x_specs + table_specs * 2 + [pl.BlockSpec(memory_space=ANY)] * (3 + len(after)),
+            in_specs=[pl.BlockSpec(memory_space=ANY)] + table_specs * 2 + [pl.BlockSpec(memory_space=ANY)] * (3 + len(after)),
             out_specs=[pl.BlockSpec(memory_space=ANY)] * 4,
             scratch_shapes=[pltpu.VMEM((2,) + w.shape[1:], jnp.bfloat16) for w in (wg, wu, wd)] +
-                           [pltpu.VMEM((rows, ff), jnp.bfloat16),
+                           [pltpu.VMEM((2, 2, slots, width), jnp.bfloat16),
+                            pltpu.VMEM((rows, ff), jnp.bfloat16),
                             pltpu.VMEM((rows, width), jnp.bfloat16),
                             pltpu.VMEM((rows // 8, 8 * width // LANES, LANES), jnp.float32),
                             pltpu.VMEM((4, acc_rows, LANES), jnp.float32),
-                            pltpu.SemaphoreType.DMA((2, 3)),
+                            pltpu.SemaphoreType.DMA((2, 5)),
                             pltpu.SemaphoreType.DMA((4,))]),
         out_shape=[acc] * 4,
         compiler_params=pltpu.CompilerParams(dimension_semantics=('arbitrary',), vmem_limit_bytes=67043328),
         cost_estimate=pl.CostEstimate(flops=2 * n_exp * rows * width * ff * 3, transcendentals=0,
                                       bytes_accessed=3 * n_exp * width * ff * 2),
         name='ffn_pass',
-    )(src, core, count, x, x, addr, addr, wt, wt, wg, wu, wd, *after)
+    )(src, core, count, x, addr, addr, wt, wt, wg, wu, wd, *after)
 
 
 def chip_sum_kernel(low_half, own_ref, sib_ref, relay_ref, out_ref):
@@ -217,12 +221,12 @@
     )(own, sib, relay)
 
 
-def final_kernel(a_ref, b_ref, *rest):
+def final_kernel(own_ref, sib_ref, a_ref, b_ref, *rest):
     out_ref, s_ref = rest[-2:]
 
     def body(b, carry):
         r = pl.ds(pl.multiple_of(b * 16 * JT, 16 * JT), 16 * JT)
-        s_ref[r, :] = a_ref[r, :] + b_ref[r, :]
+        s_ref[r, :] = (own_ref[r, :] + sib_ref[r, :]) + (a_ref[r, :] + b_ref[r, :])
         for j in range(JT):
             pair = [s_ref[pl.ds((b * 16 + k) * JT + j, 8, stride=JT), :] for k in (0, 8)]
             out_ref[pl.ds(pl.multiple_of(b * 16, 16), 16), j * LANES:(j + 1) * LANES] = (
@@ -232,22 +236,22 @@
     lax.fori_loop(0, out_ref.shape[0] // 16, body, 0, unroll=4)
 
 
-def final_sum(a, b, n, n_tok, width, out):
+def final_sum(parts, n, n_tok, width, out):
     tb = 256
     spec = pl.BlockSpec((tb * JT, LANES), lambda i: (i, 0))
     prior = [] if out is None else [out]
     return pl.pallas_call(
         final_kernel,
         grid=(n_tok // tb,),
-        in_specs=[spec, spec] + [pl.BlockSpec(memory_space=ANY)] * len(prior),
+        in_specs=[spec] * len(parts) + [pl.BlockSpec(memory_space=ANY)] * len(prior),
         out_specs=pl.BlockSpec((tb, COLS), lambda i: (i, n)),
         scratch_shapes=[pltpu.VMEM((tb * JT, LANES), jnp.float32)],
         out_shape=jax.ShapeDtypeStruct((n_tok, width), jnp.bfloat16),
-        input_output_aliases={2: 0} if prior else {},
+        input_output_aliases={len(parts): 0} if prior else {},
         compiler_params=pltpu.CompilerParams(dimension_semantics=('arbitrary',), vmem_limit_bytes=30 * 2 ** 20),
-        cost_estimate=pl.CostEstimate(flops=10 ** 7, transcendentals=0, bytes_accessed=n_tok * COLS * 10),
+        cost_estimate=pl.CostEstimate(flops=10 ** 7, transcendentals=0, bytes_accessed=n_tok * COLS * 18),
         name='final_sum',
-    )(a, b, *prior)
+    )(*parts, *prior)
 
 
 def solution(mesh):
@@ -306,8 +310,7 @@
 
         out = None
         for n, (own, sib) in zip(blocks, ffn((0, 0), gate)):
-            early = own[:n_tok * JT] + sib[:n_tok * JT] + got[n]
-            out = final_sum(early, got2[n], n, n_tok, width, out)
+            out = final_sum((own, sib, got[n], got2[n]), n, n_tok, width, out)
         return out
 
     return jax.shard_map(local_part, mesh=mesh,

time: 590 us -> 543 us (0.920)
  waiting for transfers between devices: 264 us -> 220 us
  other arithmetic: 24.7 us -> 17.9 us
    ppermute x16, waiting for transfers between devices: 259 us -> 215 us  [send(): return lax.ppermute(a, GROUP_AXES, pairs)]
    add x2 -> x0, other arithmetic: 6.98 us -> none  [local_part(): early = own[:n_tok * JT] + sib[:n_tok * JT] + got[n]]
  transfers between devices with their start and end apart: 17 -> 17, of which waited for: 8 -> 8; matrix products, arithmetic and copies ran while one was open for 3% -> 2% of each run, Pallas kernels for 2% -> 15%
where the time goes in v4:
time: 543 us
  Pallas kernels  277 us (51%)
  waiting for transfers between devices  220 us (41%)
  starting transfers between devices  18.4 us (3%)
  other arithmetic  17.9 us (3%)
  local copies, waits for them, and re-layouts  5.88 us (1%)
    pallas_call x4, Pallas kernels, ffn_pass(): pl.pallas_call(pass_kernel, grid_spec=pltpu.PrefetchScalarGridSpec(num_sc...  246 us
    ppermute x16, waiting for transfers between devices, send(): return lax.ppermute(a, GROUP_AXES, pairs)  215 us
    pallas_call x4, Pallas kernels, chip_sum(): pl.pallas_call(functools.partial(chip_sum_kernel, low_half), grid=(steps,...  22.8 us
    ppermute x16, starting transfers between devices, send(): return lax.ppermute(a, GROUP_AXES, pairs)  14.1 us
  transfers between devices with their start and end apart: 17, of which 8 were waited for; matrix products, arithmetic and copies ran while one was open for 2% of the time, Pallas kernels for 15%

profile of v4, /device:TPU:0, one launch (start us, length us, event | category | flops | bytes accessed | tf_op | source)
XLA Modules:
  0.0 542.5 jit_solution(2563808948213456970)
XLA Ops:
  0.0 2.7 fusion.5
  2.7 3.2 fusion.7
  5.9 0.1 fusion.12
  6.0 0.1 copy.14
  6.2 0.1 copy.12
  6.3 0.8 maximum_bitcast_fusion
  7.1 4.3 all-to-all-start
  11.4 0.6 pad_add_fusion.3.src_ref
  12.1 4.8 all-to-all-done
  16.9 0.1 slice_compare_fusion
  17.0 0.2 select_reduce_fusion
  17.2 0.7 reshape.33.n_ref
  17.9 0.7 slice_bitcast_fusion
  18.6 61.2 %ffn_pass.4 = (f32[8256,128]{1,0:T(8,128)}, f32[8256,128]{1,0:T(8,128)}, f32[8256,128]{1,0:T(8,128)}, f32[8256,128]{1,0:T(8,128)}) custom-call(s32[2]{0:T(128)} %pad_add_fusion.3.src_ref, s32[1]{0:T(128)} %bitcast.2.core_ref, s32[64]{0:T(128)} %reshape.33.n_ref, bf16[8,8,192,2048]{3,2,1,0:T(8,128)(2,1)} %refs_0_.7, ...), custom_call_target="tpu_custom_call" | custom-call | flops 53150220288 | bytes 138412032 | tf_op jit(solution)/shard_map/ffn_pass/pallas_call | solution.py:167
  79.9 1.6 collective-permute-start.1
  81.5 0.7 pad_add_fusion.2.src_ref
  82.2 6.5 %collective-permute-done.1 = f32[8256,128]{1,0:T(8,128)} collective-permute-done((f32[8256,128]{1,0:T(8,128)}, f32[8256,128]{1,0:T(8,128)}, u32[]{:S(2)}, u32[]{:S(2)}) %collective-permute-start.1) | collective-permute-done | bytes 4227104 | tf_op jit(solution)/shard_map/ppermute | solution.py:268
  88.6 6.1 %slice_add_fusion = (f32[4096,128]{1,0:T(8,128)}, f32[4096,128]{1,0:T(8,128)}) fusion(f32[8256,128]{1,0:T(8,128)} %collective-permute-done.1, f32[8256,128]{1,0:T(8,128)} %get-tuple-element.23), kind=kLoop, calls=%fused_computation.9 | loop fusion | flops 1048576 | bytes 12582912 | tf_op jit(solution)/shard_map/add | solution.py:295
  94.7 4.8 slice_add_fusion.1
  99.5 61.4 %ffn_pass.5 = (f32[8256,128]{1,0:T(8,128)}, f32[8256,128]{1,0:T(8,128)}, f32[8256,128]{1,0:T(8,128)}, f32[8256,128]{1,0:T(8,128)}) custom-call(s32[2]{0:T(128)} %pad_add_fusion.2.src_ref, s32[1]{0:T(128)} %bitcast.2.core_ref, s32[64]{0:T(128)} %reshape.33.n_ref, bf16[8,8,192,2048]{3,2,1,0:T(8,128)(2,1)} %refs_0_.7, ...), custom_call_target="tpu_custom_call" | custom-call | flops 53150220288 | bytes 138412032 | tf_op jit(solution)/shard_map/ffn_pass/pallas_call | solution.py:167
  160.9 2.5 collective-permute-start.4
  163.5 2.0 collective-permute-start.3
  165.5 0.6 pad_add_fusion.1.src_ref
  166.1 23.7 %collective-permute-done.5.relay_ref = f32[4096,128]{1,0:T(8,128)} collective-permute-done((f32[4096,128]{1,0:T(8,128)}, f32[4096,128]{1,0:T(8,128)}, u32[]{:S(2)}, u32[]{:S(2)}) %collective-permute-start.5) | collective-permute-done | bytes 2097184 | tf_op jit(solution)/shard_map/ppermute | solution.py:268
  189.8 5.8 %chip_sum.5.refs_9_ = f32[8192,128]{1,0:T(8,128)} custom-call(f32[8256,128]{1,0:T(8,128)} %get-tuple-element.27.own_ref, f32[8256,128]{1,0:T(8,128)} %collective-permute-done.4.sib_ref, f32[4096,128]{1,0:T(8,128)} %collective-permute-done.5.relay_ref), custom_call_target="tpu_custom_call" | custom-call | flops 10000000 | bytes 14680064 | tf_op jit(solution)/shard_map/chip_sum/pallas_call | solution.py:212
  195.6 16.6 %collective-permute-done.3.relay_ref = f32[4096,128]{1,0:T(8,128)S(1)} collective-permute-done((f32[4096,128]{1,0:T(8,128)}, f32[4096,128]{1,0:T(8,128)S(1)}, u32[]{:S(2)}, u32[]{:S(2)}) %collective-permute-start.3) | collective-permute-done | bytes 2097184 | tf_op jit(solution)/shard_map/ppermute | solution.py:268
  212.2 1.3 copy-done.4
  213.5 5.7 %chip_sum.4.refs_8_ = f32[8192,128]{1,0:T(8,128)} custom-call(f32[8256,128]{1,0:T(8,128)} %get-tuple-element.25.own_ref, f32[8256,128]{1,0:T(8,128)} %collective-permute-done.2.sib_ref, f32[4096,128]{1,0:T(8,128)} %copy-done.4), custom_call_target="tpu_custom_call" | custom-call | flops 10000000 | bytes 14680064 | tf_op jit(solution)/shard_map/chip_sum/pallas_call | solution.py:212
  219.2 61.6 %ffn_pass.6 = (f32[8256,128]{1,0:T(8,128)}, f32[8256,128]{1,0:T(8,128)}, f32[8256,128]{1,0:T(8,128)}, f32[8256,128]{1,0:T(8,128)}) custom-call(s32[2]{0:T(128)} %pad_add_fusion.1.src_ref, s32[1]{0:T(128)} %bitcast.2.core_ref, s32[64]{0:T(128)} %reshape.33.n_ref, bf16[8,8,192,2048]{3,2,1,0:T(8,128)(2,1)} %refs_0_.7, ...), custom_call_target="tpu_custom_call" | custom-call | flops 53150220288 | bytes 138412032 | tf_op jit(solution)/shard_map/ffn_pass/pallas_call | solution.py:167
  280.8 1.7 collective-permute-start.8
  282.5 0.1 collective-permute-start.9
  282.6 1.9 collective-permute-start.7
  284.5 0.6 pad_add_fusion.src_ref
  285.1 0.1 collective-permute-start.14
  285.3 23.6 %collective-permute-done.9.relay_ref = f32[4096,128]{1,0:T(8,128)} collective-permute-done((f32[4096,128]{1,0:T(8,128)}, f32[4096,128]{1,0:T(8,128)}, u32[]{:S(2)}, u32[]{:S(2)}) %collective-permute-start.9) | collective-permute-done | bytes 2097184 | tf_op jit(solution)/shard_map/ppermute | solution.py:268
  308.8 5.6 %chip_sum.7.refs_9_ = f32[8192,128]{1,0:T(8,128)} custom-call(f32[8256,128]{1,0:T(8,128)} %get-tuple-element.31.own_ref, f32[8256,128]{1,0:T(8,128)} %collective-permute-done.8.sib_ref, f32[4096,128]{1,0:T(8,128)} %collective-permute-done.9.relay_ref), custom_call_target="tpu_custom_call" | custom-call | flops 10000000 | bytes 14680064 | tf_op jit(solution)/shard_map/chip_sum/pallas_call | solution.py:212
  314.5 16.7 %collective-permute-done.7.relay_ref = f32[4096,128]{1,0:T(8,128)S(1)} collective-permute-done((f32[4096,128]{1,0:T(8,128)}, f32[4096,128]{1,0:T(8,128)S(1)}, u32[]{:S(2)}, u32[]{:S(2)}) %collective-permute-start.7) | collective-permute-done | bytes 2097184 | tf_op jit(solution)/shard_map/ppermute | solution.py:268
  331.2 1.3 copy-done.3
  332.5 5.7 %chip_sum.6.refs_8_ = f32[8192,128]{1,0:T(8,128)} custom-call(f32[8256,128]{1,0:T(8,128)} %get-tuple-element.29.own_ref, f32[8256,128]{1,0:T(8,128)} %collective-permute-done.6.sib_ref, f32[4096,128]{1,0:T(8,128)} %copy-done.3), custom_call_target="tpu_custom_call" | custom-call | flops 10000000 | bytes 14680064 | tf_op jit(solution)/shard_map/chip_sum/pallas_call | solution.py:212
  338.2 61.5 %ffn_pass.7 = (f32[8256,128]{1,0:T(8,128)}, f32[8256,128]{1,0:T(8,128)}, f32[8256,128]{1,0:T(8,128)}, f32[8256,128]{1,0:T(8,128)}) custom-call(s32[2]{0:T(128)} %pad_add_fusion.src_ref, s32[1]{0:T(128)} %bitcast.2.core_ref, s32[64]{0:T(128)} %reshape.33.n_ref, bf16[8,8,192,2048]{3,2,1,0:T(8,128)(2,1)} %refs_0_.7, ...), custom_call_target="tpu_custom_call" | custom-call | flops 53150220288 | bytes 138412032 | tf_op jit(solution)/shard_map/ffn_pass/pallas_call | solution.py:167
  399.7 1.7 collective-permute-start.13
  401.4 1.6 collective-permute-start.11
  403.0 0.7 collective-permute-start.12
  403.7 90.9 %collective-permute-done.15.b_ref = f32[8192,128]{1,0:T(8,128)S(1)} collective-permute-done((f32[8192,128]{1,0:T(8,128)}, f32[8192,128]{1,0:T(8,128)S(1)}, u32[]{:S(2)}, u32[]{:S(2)}) %collective-permute-start.15) | collective-permute-done | bytes 4194336 | tf_op jit(solution)/shard_map/ppermute | solution.py:268
  494.6 2.2 copy-done
  496.8 5.2 final_sum.2.rest_0_
  502.0 37.5 %collective-permute-done.12.b_ref = f32[8192,128]{1,0:T(8,128)S(1)} collective-permute-done((f32[8192,128]{1,0:T(8,128)}, f32[8192,128]{1,0:T(8,128)S(1)}, u32[]{:S(2)}, u32[]{:S(2)}) %collective-permute-start.12) | collective-permute-done | bytes 4194336 | tf_op jit(solution)/shard_map/ppermute | solution.py:268
  539.5 3.0 final_sum.3
  (29 shorter events, 0.3 us)
Async XLA Ops:
  0.0 2.7 copy-start.5
  7.1 9.8 %all-to-all-start = ((f32[8,2,8,192]{3,1,2,0:T(2,128)}), f32[8,2,8,192]{3,1,2,0:T(2,128)S(1)}, u32[]{:S(2)}, u32[]{:S(2)}) async-start(f32[8,2,8,192]{3,1,2,0:T(2,128)} %maximum_bitcast_fusion), calls=%async_computation | async-start | bytes 262144 | tf_op jit(solution)/shard_map/all_to_all | solution.py:278
  79.9 8.8 %collective-permute-start.1 = (f32[8256,128]{1,0:T(8,128)}, f32[8256,128]{1,0:T(8,128)}, u32[]{:S(2)}, u32[]{:S(2)}) collective-permute-start(f32[8256,128]{1,0:T(8,128)} %get-tuple-element.24), channel_id=1, source_target_pairs={{0,1},{1,0},{2,3},{3,2},{4,5},{5,4},{6,7},{7,6}} | collective-permute-start | bytes 12681224 | tf_op jit(solution)/shard_map/ppermute | solution.py:268
  81.5 13.3 %collective-permute-start = (f32[8256,128]{1,0:T(8,128)}, f32[8256,128]{1,0:T(8,128)}, u32[]{:S(2)}, u32[]{:S(2)}) collective-permute-start(f32[8256,128]{1,0:T(8,128)} %get-tuple-element.22), channel_id=1, source_target_pairs={{0,1},{1,0},{2,3},{3,2},{4,5},{5,4},{6,7},{7,6}} | collective-permute-start | bytes 12681224 | tf_op jit(solution)/shard_map/ppermute | solution.py:268
  88.6 6.1 %copy-start.2 = (f32[8256,128]{1,0:T(8,128)S(1)}, f32[8256,128]{1,0:T(8,128)}, u32[]{:S(2)}) copy-start(f32[8256,128]{1,0:T(8,128)} %get-tuple-element.21) | copy-start | bytes 12681220
  160.9 28.9 %collective-permute-start.4 = (f32[8256,128]{1,0:T(8,128)}, f32[8256,128]{1,0:T(8,128)}, u32[]{:S(2)}, u32[]{:S(2)}) collective-permute-start(f32[8256,128]{1,0:T(8,128)} %get-tuple-element.28), channel_id=1, source_target_pairs={{0,1},{1,0},{2,3},{3,2},{4,5},{5,4},{6,7},{7,6}} | collective-permute-start | bytes 12681224 | tf_op jit(solution)/shard_map/ppermute | solution.py:268
  163.4 48.8 %collective-permute-start.2 = (f32[8256,128]{1,0:T(8,128)}, f32[8256,128]{1,0:T(8,128)}, u32[]{:S(2)}, u32[]{:S(2)}) collective-permute-start(f32[8256,128]{1,0:T(8,128)} %get-tuple-element.26), channel_id=1, source_target_pairs={{0,1},{1,0},{2,3},{3,2},{4,5},{5,4},{6,7},{7,6}} | collective-permute-start | bytes 12681224 | tf_op jit(solution)/shard_map/ppermute | solution.py:268
  163.5 26.4 %collective-permute-start.5 = (f32[4096,128]{1,0:T(8,128)}, f32[4096,128]{1,0:T(8,128)}, u32[]{:S(2)}, u32[]{:S(2)}) collective-permute-start(f32[4096,128]{1,0:T(8,128)} %get-tuple-element.37), channel_id=1, source_target_pairs={{0,4},{1,3},{2,6},{3,1},{4,0},{5,7},{6,2},{7,5}} | collective-permute-start | bytes 6291464 | tf_op jit(solution)/shard_map/ppermute | solution.py:268
  163.5 48.7 %collective-permute-start.3 = (f32[4096,128]{1,0:T(8,128)}, f32[4096,128]{1,0:T(8,128)S(1)}, u32[]{:S(2)}, u32[]{:S(2)}) collective-permute-start(f32[4096,128]{1,0:T(8,128)} %get-tuple-element.39), channel_id=1, source_target_pairs={{0,4},{1,3},{2,6},{3,1},{4,0},{5,7},{6,2},{7,5}} | collective-permute-start | bytes 6291464 | tf_op jit(solution)/shard_map/ppermute | solution.py:268
  212.2 1.3 copy-start.4
  280.8 28.1 %collective-permute-start.8 = (f32[8256,128]{1,0:T(8,128)}, f32[8256,128]{1,0:T(8,128)}, u32[]{:S(2)}, u32[]{:S(2)}) collective-permute-start(f32[8256,128]{1,0:T(8,128)} %get-tuple-element.32), channel_id=1, source_target_pairs={{0,1},{1,0},{2,3},{3,2},{4,5},{5,4},{6,7},{7,6}} | collective-permute-start | bytes 12681224 | tf_op jit(solution)/shard_map/ppermute | solution.py:268
  282.4 48.8 %collective-permute-start.6 = (f32[8256,128]{1,0:T(8,128)}, f32[8256,128]{1,0:T(8,128)}, u32[]{:S(2)}, u32[]{:S(2)}) collective-permute-start(f32[8256,128]{1,0:T(8,128)} %get-tuple-element.30), channel_id=1, source_target_pairs={{0,1},{1,0},{2,3},{3,2},{4,5},{5,4},{6,7},{7,6}} | collective-permute-start | bytes 12681224 | tf_op jit(solution)/shard_map/ppermute | solution.py:268
  282.5 26.4 %collective-permute-start.9 = (f32[4096,128]{1,0:T(8,128)}, f32[4096,128]{1,0:T(8,128)}, u32[]{:S(2)}, u32[]{:S(2)}) collective-permute-start(f32[4096,128]{1,0:T(8,128)} %get-tuple-element.38.refs_9_), channel_id=1, source_target_pairs={{0,2},{1,5},{2,0},{3,7},{4,6},{5,1},{6,4},{7,3}} | collective-permute-start | bytes 6291464 | tf_op jit(solution)/shard_map/ppermute | solution.py:268
  282.6 48.6 %collective-permute-start.7 = (f32[4096,128]{1,0:T(8,128)}, f32[4096,128]{1,0:T(8,128)S(1)}, u32[]{:S(2)}, u32[]{:S(2)}) collective-permute-start(f32[4096,128]{1,0:T(8,128)} %get-tuple-element.40.refs_8_), channel_id=1, source_target_pairs={{0,2},{1,5},{2,0},{3,7},{4,6},{5,1},{6,4},{7,3}} | collective-permute-start | bytes 6291464 | tf_op jit(solution)/shard_map/ppermute | solution.py:268
  285.1 117.9 %collective-permute-start.14 = (f32[8192,128]{1,0:T(8,128)}, f32[8192,128]{1,0:T(8,128)}, u32[]{:S(2)}, u32[]{:S(2)}) collective-permute-start(f32[8192,128]{1,0:T(8,128)} %chip_sum.4.refs_8_), channel_id=1, source_target_pairs={{0,2},{1,5},{2,0},{3,7},{4,6},{5,1},{6,4},{7,3}} | collective-permute-start | bytes 12582920 | tf_op jit(solution)/shard_map/ppermute | solution.py:268
  331.2 1.3 copy-start.3
  399.7 94.9 %collective-permute-start.13 = (f32[8256,128]{1,0:T(8,128)}, f32[8256,128]{1,0:T(8,128)S(1)}, u32[]{:S(2)}, u32[]{:S(2)}) collective-permute-start(f32[8256,128]{1,0:T(8,128)} %get-tuple-element.36), channel_id=1, source_target_pairs={{0,1},{1,0},{2,3},{3,2},{4,5},{5,4},{6,7},{7,6}} | collective-permute-start | bytes 12681224 | tf_op jit(solution)/shard_map/ppermute | solution.py:268
  401.4 138.1 %collective-permute-start.10 = (f32[8256,128]{1,0:T(8,128)}, f32[8256,128]{1,0:T(8,128)S(1)}, u32[]{:S(2)}, u32[]{:S(2)}) collective-permute-start(f32[8256,128]{1,0:T(8,128)} %get-tuple-element.34), channel_id=1, source_target_pairs={{0,1},{1,0},{2,3},{3,2},{4,5},{5,4},{6,7},{7,6}} | collective-permute-start | bytes 12681224 | tf_op jit(solution)/shard_map/ppermute | solution.py:268
  401.4 93.2 %collective-permute-start.15 = (f32[8192,128]{1,0:T(8,128)}, f32[8192,128]{1,0:T(8,128)S(1)}, u32[]{:S(2)}, u32[]{:S(2)}) collective-permute-start(f32[8192,128]{1,0:T(8,128)} %chip_sum.6.refs_8_), channel_id=1, source_target_pairs={{0,4},{1,3},{2,6},{3,1},{4,0},{5,7},{6,2},{7,5}} | collective-permute-start | bytes 12582920 | tf_op jit(solution)/shard_map/ppermute | solution.py:268
  401.4 100.6 %collective-permute-start.11 = (f32[8192,128]{1,0:T(8,128)}, f32[8192,128]{1,0:T(8,128)S(1)}, u32[]{:S(2)}, u32[]{:S(2)}) collective-permute-start(f32[8192,128]{1,0:T(8,128)} %chip_sum.5.refs_9_), channel_id=1, source_target_pairs={{0,2},{1,5},{2,0},{3,7},{4,6},{5,1},{6,4},{7,3}} | collective-permute-start | bytes 12582920 | tf_op jit(solution)/shard_map/ppermute | solution.py:268
  403.0 136.5 %collective-permute-start.12 = (f32[8192,128]{1,0:T(8,128)}, f32[8192,128]{1,0:T(8,128)S(1)}, u32[]{:S(2)}, u32[]{:S(2)}) collective-permute-start(f32[8192,128]{1,0:T(8,128)} %chip_sum.7.refs_9_), channel_id=1, source_target_pairs={{0,4},{1,3},{2,6},{3,1},{4,0},{5,7},{6,2},{7,5}} | collective-permute-start | bytes 12582920 | tf_op jit(solution)/shard_map/ppermute | solution.py:268
  494.6 2.2 copy-start
  496.8 42.7 %copy-start.1 = (f32[8256,128]{1,0:T(8,128)S(1)}, f32[8256,128]{1,0:T(8,128)}, u32[]{:S(2)}) copy-start(f32[8256,128]{1,0:T(8,128)} %get-tuple-element.33.own_ref) | copy-start | bytes 12681220
